TPU v7x, 128 devices: a whole 4x4x4 slice. The times are simulated.
128 devices in a mesh: seq: 16 (over z, x), head: 8 (over y, core).
Axes of the slice: x: 4, y: 4, z: 4, core: 2. Of those that a mesh axis runs over, the one named last changes fastest.
Arguments:
- context: bfloat16 [32768, 2048], P('seq'), may hold values from -64 to 64
- wq_cross: bfloat16 [2048, 2048], P(None, 'head'), may hold values from -4 to 4
- wk_cross: bfloat16 [2048, 2048], P(None, 'head'), may hold values from -4 to 4
- wv_cross: bfloat16 [2048, 2048], P(None, 'head'), may hold values from -0.125 to 0.125
- wo_cross: bfloat16 [2048, 2048], P('head'), may hold values from -0.125 to 0.125
- wq_latent: bfloat16 [2048, 2048], P(None, 'head'), may hold values from -4 to 4
- wk_latent: bfloat16 [2048, 2048], P(None, 'head'), may hold values from -4 to 4
- wv_latent: bfloat16 [2048, 2048], P(None, 'head'), may hold values from -0.125 to 0.125
- wo_latent: bfloat16 [2048, 2048], P('head'), may hold values from -0.125 to 0.125
- cross_keep: int32 [16, 2048, 4096], P('head', None, 'seq'), may hold values from 0 to 255, as said below
- latent_keep: int32 [16, 2048, 128], P('head'), may hold values from 0 to 65535, as said below
- residual_keep: int32 [2, 2048, 128], replicated, may hold values from 0 to 65535, as said below
Outputs:
- latents_out: bfloat16 [2048, 2048], P('seq', 'head')
Inputs may be any that keep to these rules, and one draw needn't show every extreme that they name: `cross_keep`: each of the 8 low bits of a word is one keep flag, laid out as the steps say. `latent_keep`: each of the 16 low bits of a word is one keep flag, laid out as the steps say. `residual_keep`: each of the 16 low bits of a word is one keep flag, laid out as the steps say.
All inputs are finite; a program needn't handle non-finite values.
Results may differ from a plain program's by a relative error of at most 0.015.
Values may be sent and summed in bfloat16 or wider, within the bound.
No kernel may reach another device: no remote copies, remote signals or barrier semaphores. Data moves between devices by JAX's collectives and lax.ppermute only.
A program may use at most 128 MiB of HBM per device.

v0:
```python
import math

import jax
import jax.numpy as jnp
from jax import lax
from jax.experimental import pallas as pl
from jax.experimental.pallas import tpu as pltpu
from jax.sharding import PartitionSpec as P


bf16 = jnp.bfloat16
f32 = jnp.float32
keep_scale = 8.0 / 7.0
masked = -1e30
head_dim = 128
query_scale = math.log2(math.e) / math.sqrt(head_dim)
stat_rows = 16


def params(limit=48):
    return pltpu.CompilerParams(
        dimension_semantics=("arbitrary",), vmem_limit_bytes=limit * 1024 * 1024
    )


def row_scale(rows):
    wide = rows.astype(f32)
    mean_square = jnp.mean(wide * wide, axis=-1, keepdims=True)
    return lax.rsqrt(mean_square + 1e-06)


def query_kernel(root, where_ref, x_ref, w_ref, out_ref):
    @pl.when(where_ref[0] == root)
    def _():
        x = x_ref[...]
        product = jnp.dot(x, w_ref[...], preferred_element_type=f32)
        out_ref[...] = (
            (product * (row_scale(x) * query_scale)).astype(bf16).reshape(out_ref.shape)
        )


def query_chunks(where, context, wq, seq_count):
    tok_rows, width = context.shape
    columns = wq.shape[1]
    rows = tok_rows // seq_count
    group = 4
    root = seq_count - 1
    spec = pltpu.PrefetchScalarGridSpec(
        num_scalar_prefetch=1,
        grid=(seq_count // group,),
        in_specs=[
            pl.BlockSpec((rows * group, width), lambda i, at: (jnp.where(at[0] == root, i, 0), 0)),
            pl.BlockSpec((width, columns), lambda i, at: (0, 0)),
        ],
        out_specs=pl.BlockSpec((group, rows, columns), lambda i, at: (i, 0, 0)),
    )
    return pl.pallas_call(
        lambda *refs: query_kernel(root, *refs),
        grid_spec=spec,
        out_shape=jax.ShapeDtypeStruct((seq_count, rows, columns), bf16),
        compiler_params=params(52),
        name="queries",
    )(where, context, wq)


def kv_kernel(x_ref, wk_ref, wv_ref, k_ref, v_ref):
    x = x_ref[...]
    scale = row_scale(x)
    k_ref[...] = (jnp.dot(x, wk_ref[...], preferred_element_type=f32) * scale).astype(bf16)
    v_ref[...] = (jnp.dot(x, wv_ref[...], preferred_element_type=f32) * scale).astype(bf16)


def keys_values(context, wk, wv):
    tok_rows, width = context.shape
    columns = wk.shape[1]
    block = 512
    return pl.pallas_call(
        kv_kernel,
        grid=(tok_rows // block,),
        in_specs=[
            pl.BlockSpec((block, width), lambda i: (i, 0)),
            pl.BlockSpec((width, columns), lambda i: (0, 0)),
            pl.BlockSpec((width, columns), lambda i: (0, 0)),
        ],
        out_specs=[pl.BlockSpec((block, columns), lambda i: (i, 0))] * 2,
        out_shape=[jax.ShapeDtypeStruct((tok_rows, columns), bf16)] * 2,
        compiler_params=params(52),
        name="keys_values",
    )(context, wk, wv)


def softmax_rows(scores_of, keep_of, values_of, pieces):
    scores = [scores_of(b) for b in range(pieces)]
    top = scores[0]
    for s in scores[1:]:
        top = jnp.maximum(top, s)
    top = jnp.max(top, axis=-1, keepdims=True)
    total = None
    summed = None
    for b in range(pieces):
        p = jnp.exp2(scores[b] - top)
        total = p if total is None else total + p
        kept = jnp.where(keep_of(b), p, 0.0).astype(bf16)
        part = jnp.dot(kept, values_of(b), preferred_element_type=f32)
        summed = part if summed is None else summed + part
    total = jnp.sum(total, axis=-1, keepdims=True)
    return summed, top, total


def nt_dot(a, b):
    return lax.dot_general(a, b, (((1,), (1,)), ((), ())), preferred_element_type=f32)


def cross_kernel(
    root, n, steps, where_ref, q_ref, k_ref, v_ref, words_ref, out_ref, s0_ref, s1_ref, m_ref
):
    rows = n * head_dim
    wide = words_ref.shape[2]
    step = pl.program_id(0)
    following = jnp.minimum(step + 1, steps - 1)

    def score(head, block, b, causal):
        cols = slice(head * head_dim, (head + 1) * head_dim)
        q = q_ref[pl.ds(block * n, n), :, cols].reshape(rows, head_dim)
        s = nt_dot(q, k_ref[b * wide : (b + 1) * wide, cols])
        if causal and (b + 1) * wide > block * rows:
            key = b * wide + lax.broadcasted_iota(jnp.int32, s.shape, 1)
            row = block * rows + lax.broadcasted_iota(jnp.int32, s.shape, 0)
            s = jnp.where(key <= row, s, masked)
        return s

    def stage(head, next_block, pieces, next_pieces, causal):
        ready, filling = (s0_ref, s1_ref) if head == 0 else (s1_ref, s0_ref)
        cols = slice(head * head_dim, (head + 1) * head_dim)
        words = words_ref[head].astype(jnp.int16)
        top = jnp.max(m_ref[head], axis=-1, keepdims=True)
        total = None
        summed = None
        next_top = None
        for b in range(max(pieces, next_pieces)):
            if b < next_pieces:
                s = score(1 - head, next_block, b, causal)
            if b < pieces:
                p = jnp.exp2(ready[b] - top)
                total = p if total is None else total + p
                kept = jnp.where(
                    (words & jnp.int16(1 << b)) != jnp.int16(0), p.astype(bf16), bf16(0)
                )
                part = jnp.dot(
                    kept, v_ref[b * wide : (b + 1) * wide, cols], preferred_element_type=f32
                )
                summed = part if summed is None else summed + part
            if b < next_pieces:
                filling[b] = s
                next_top = s if next_top is None else jnp.maximum(next_top, s)
        if next_pieces:
            m_ref[1 - head] = next_top
        total = jnp.sum(total, axis=-1, keepdims=True)
        out = (summed * (keep_scale / total)).astype(bf16)
        for i in range(n):
            out_ref[i, head * head_dim : (head + 1) * head_dim, :] = out[
                i * head_dim : (i + 1) * head_dim
            ]
        return top + jnp.log2(total)

    def first_scores(pieces, causal):
        first_top = None
        for b in range(pieces):
            s = score(0, 0, b, causal)
            s0_ref[b] = s
            first_top = s if first_top is None else jnp.maximum(first_top, s)
        m_ref[0] = first_top

    def run(block, next_block, pieces, next_pieces, causal):
        sums = [
            stage(0, block, pieces, pieces, causal),
            stage(1, next_block, pieces, next_pieces, causal),
        ]
        lanes = lax.broadcasted_iota(jnp.int32, (rows, head_dim), 1)
        stats = jnp.zeros((rows, head_dim), f32)
        for head, lse in enumerate(sums):
            high = lse.astype(bf16).astype(f32)
            middle = (lse - high).astype(bf16).astype(f32)
            low = lse - high - middle
            for j, piece in enumerate((high, middle, low)):
                stats = jnp.where(lanes == head * 3 + j, piece, stats)
        for i in range(n):
            out_ref[i, 2 * head_dim :, :] = (
                stats[i * head_dim : (i + 1) * head_dim].T[:stat_rows].astype(bf16)
            )

    for k in range(steps):

        @pl.when((where_ref[0] == root) & (step == k))
        def _():
            reach = [(j + 1) * rows // wide for j in range(steps)] + [0]
            if k == 0:
                first_scores(reach[0], True)
            run(k, k + 1, reach[k], reach[k + 1], True)

    @pl.when(where_ref[0] != root)
    def _():
        @pl.when(step == 0)
        def _():
            first_scores(8, False)

        run(step, following, 8, 8, False)


def cross_attention(where, queries, keys, values, words, root):
    count = queries.shape[0]
    n = 4
    rows = n * head_dim
    wide = words.shape[2]
    whole = pl.Buffered(1)
    spec = pltpu.PrefetchScalarGridSpec(
        num_scalar_prefetch=1,
        grid=(count // n,),
        in_specs=[
            pl.BlockSpec(queries.shape, lambda i, at: (0, 0, 0), pipeline_mode=whole),
            pl.BlockSpec(keys.shape, lambda i, at: (0, 0), pipeline_mode=whole),
            pl.BlockSpec(values.shape, lambda i, at: (0, 0), pipeline_mode=whole),
            pl.BlockSpec((2, rows, wide), lambda i, at: (0, i, 0)),
        ],
        out_specs=pl.BlockSpec((n, 2 * head_dim + stat_rows, head_dim), lambda i, at: (i, 0, 0)),
        scratch_shapes=[
            pltpu.VMEM((8, rows, wide), f32),
            pltpu.VMEM((8, rows, wide), f32),
            pltpu.VMEM((2, rows, wide), f32),
        ],
    )
    return pl.pallas_call(
        lambda *refs: cross_kernel(root, n, count // n, *refs),
        grid_spec=spec,
        out_shape=jax.ShapeDtypeStruct((count, 2 * head_dim + stat_rows, head_dim), bf16),
        compiler_params=params(52),
        cost_estimate=pl.CostEstimate(
            flops=8 * count * head_dim * keys.shape[0] * head_dim,
            transcendentals=2 * count * head_dim * keys.shape[0],
            bytes_accessed=4 * words.size,
        ),
        name="cross_attention",
    )(where, queries, keys, values, words)


def project_shares(attended, wo_ref, core, own_ref, theirs_ref):
    columns = own_ref.shape[2]
    for p in range(own_ref.shape[0]):
        for side, out_ref in ((core, own_ref), (1 - core, theirs_ref)):
            first = pl.multiple_of((2 * p + side) * columns, columns)
            share = jnp.dot(
                attended, wo_ref[:, pl.ds(first, columns)], preferred_element_type=f32
            )
            out_ref[p] = share.astype(out_ref.dtype)


def share_shapes(pairs, rows, columns):
    return [
        jax.ShapeDtypeStruct((pairs, rows, columns), f32),
        jax.ShapeDtypeStruct((pairs, rows, columns), bf16),
    ]


def combine_kernel(where_ref, parts_ref, wo_ref, own_ref, theirs_ref):
    count = parts_ref.shape[0]
    rows = head_dim
    heads = []
    stats = parts_ref[:, 2 * rows :, :].astype(f32)
    for head in range(2):
        lse = stats[:, head * 3] + stats[:, head * 3 + 1] + stats[:, head * 3 + 2]
        weight = jnp.exp2(lse - jnp.max(lse, axis=0, keepdims=True))
        weight = weight / jnp.sum(weight, axis=0, keepdims=True)
        weight = jnp.concatenate([weight, jnp.zeros((rows - count, rows), f32)], axis=0).T
        mixed = None
        for s in range(count):
            part = parts_ref[s, head * rows : (head + 1) * rows, :].astype(f32)
            part = part * weight[:, s : s + 1]
            mixed = part if mixed is None else mixed + part
        heads.append(mixed.astype(bf16))
    attended = jnp.concatenate(heads, axis=1)
    project_shares(attended, wo_ref, where_ref[1] % 2, own_ref, theirs_ref)


def combine(where, parts, wo, pairs):
    whole = lambda i, at: (0, 0, 0)
    spec = pltpu.PrefetchScalarGridSpec(
        num_scalar_prefetch=1,
        grid=(1,),
        in_specs=[
            pl.BlockSpec(parts.shape, whole),
            pl.BlockSpec(wo.shape, lambda i, at: (0, 0)),
        ],
        out_specs=[pl.BlockSpec((pairs, head_dim, 256), whole)] * 2,
    )
    return pl.pallas_call(
        combine_kernel,
        grid_spec=spec,
        out_shape=share_shapes(pairs, head_dim, 256),
        compiler_params=params(16),
        name="combine",
    )(where, parts, wo)


def chip_sum_kernel(where_ref, own_ref, got_ref, kept_ref, *out_refs):
    pairs = own_ref.shape[0]
    place = where_ref[1] // 2
    kept_ref[...] = own_ref[place] + got_ref[place].astype(f32)
    for d, out_ref in enumerate(out_refs, 1):
        target = lax.rem(place + d, pairs)
        out_ref[...] = (own_ref[target] + got_ref[target].astype(f32)).astype(bf16)


def chip_sum(where, own, got):
    pairs, rows, columns = own.shape
    flat = lambda i, at: (0, 0)
    spec = pltpu.PrefetchScalarGridSpec(
        num_scalar_prefetch=1,
        grid=(1,),
        in_specs=[pl.BlockSpec(own.shape, lambda i, at: (0, 0, 0))] * 2,
        out_specs=[pl.BlockSpec((rows, columns), flat)] * pairs,
    )
    return pl.pallas_call(
        chip_sum_kernel,
        grid_spec=spec,
        out_shape=[jax.ShapeDtypeStruct((rows, columns), f32)]
        + [jax.ShapeDtypeStruct((rows, columns), bf16)] * (pairs - 1),
        compiler_params=params(8),
        name="chip_sum",
    )(where, own, got)


def residual_kernel(where_ref, *refs):
    *share_refs, base_ref, words_ref, out_ref = refs
    total = share_refs[0][...].astype(f32)
    for ref in share_refs[1:]:
        total = total + ref[...].astype(f32)
    words = words_ref[0]
    for half in range(2):
        cols = slice(half * 128, half * 128 + 128)
        flag = (jnp.right_shift(words, where_ref[1] * 2 + half) & 1).astype(f32)
        base = base_ref[:, cols].astype(f32)
        out_ref[:, cols] = (base + flag * keep_scale * total[:, cols]).astype(bf16)


def residual(where, shares, base, words, index):
    rows, columns = base.shape
    flat = lambda i, at: (0, 0)
    spec = pltpu.PrefetchScalarGridSpec(
        num_scalar_prefetch=1,
        grid=(1,),
        in_specs=[pl.BlockSpec((rows, columns), flat)] * (len(shares) + 1)
        + [pl.BlockSpec((1, rows, 128), lambda i, at: (index, at[0], 0))],
        out_specs=pl.BlockSpec((rows, columns), flat),
    )
    return pl.pallas_call(
        residual_kernel,
        grid_spec=spec,
        out_shape=jax.ShapeDtypeStruct((rows, columns), bf16),
        compiler_params=params(8),
        name="residual",
    )(where, *shares, base, words)


def latent_qkv_kernel(where_ref, near_ref, far_ref, wq_ref, wk_ref, wv_ref, q_ref, kv_ref):
    pairs, _, columns = near_ref.shape
    place = where_ref[1] // 2
    core = where_ref[1] % 2
    pieces = []
    for d in range(pairs):
        chip = lax.rem(place + pairs - d, pairs)
        for ref, side in ((near_ref, core), (far_ref, 1 - core)):
            first = pl.multiple_of((2 * chip + side) * columns, columns)
            pieces.append((ref[d], first))
    squares = None
    for piece, _ in pieces:
        wide = piece.astype(f32)
        part = jnp.sum(wide * wide, axis=-1, keepdims=True)
        squares = part if squares is None else squares + part
    scale = lax.rsqrt(squares / (2 * pairs * columns) + 1e-06)

    def project(w_ref):
        total = None
        for piece, first in pieces:
            part = jnp.dot(piece, w_ref[pl.ds(first, columns), :], preferred_element_type=f32)
            total = part if total is None else total + part
        return total * scale

    q_ref[...] = (project(wq_ref) * query_scale).astype(bf16)
    keys = project(wk_ref).astype(bf16)
    values = project(wv_ref).astype(bf16)
    for s in range(kv_ref.shape[0]):
        kv_ref[s, :, :columns] = keys
        kv_ref[s, :, columns:] = values


def latent_qkv(where, near, far, wq, wk, wv, seq_count):
    _, rows, columns = near.shape
    spec = pltpu.PrefetchScalarGridSpec(
        num_scalar_prefetch=1,
        grid=(1,),
        in_specs=[pl.BlockSpec(near.shape, lambda i, at: (0, 0, 0))] * 2
        + [pl.BlockSpec(wq.shape, lambda i, at: (0, 0))] * 3,
        out_specs=[
            pl.BlockSpec((rows, columns), lambda i, at: (0, 0)),
            pl.BlockSpec((seq_count, rows, 2 * columns), lambda i, at: (0, 0, 0)),
        ],
    )
    return pl.pallas_call(
        latent_qkv_kernel,
        grid_spec=spec,
        out_shape=[
            jax.ShapeDtypeStruct((rows, columns), bf16),
            jax.ShapeDtypeStruct((seq_count, rows, 2 * columns), bf16),
        ],
        compiler_params=params(24),
        name="latent_qkv",
    )(where, near, far, wq, wk, wv)


def latent_kernel(where_ref, q_ref, kv_ref, words_ref, wo_ref, own_ref, theirs_ref):
    count, rows, _ = kv_ref.shape
    heads = []
    for head in range(2):
        cols = slice(head * head_dim, (head + 1) * head_dim)
        value_cols = slice(256 + head * head_dim, 256 + (head + 1) * head_dim)
        q = q_ref[:, cols]
        words = words_ref[head]

        def scores_of(t):
            s = nt_dot(q, kv_ref[t, :, cols])
            key = t * rows + lax.broadcasted_iota(jnp.int32, s.shape, 1)
            row = where_ref[0] * rows + lax.broadcasted_iota(jnp.int32, s.shape, 0)
            return jnp.where(key <= row, s, masked)

        summed, _, total = softmax_rows(
            scores_of,
            lambda t: (words & (1 << t)) != 0,
            lambda t: kv_ref[t, :, value_cols],
            count,
        )
        heads.append((summed * (keep_scale / total)).astype(bf16))
    attended = jnp.concatenate(heads, axis=1)
    project_shares(attended, wo_ref, where_ref[1] % 2, own_ref, theirs_ref)


def latent_attention(where, q, kv, words, wo, pairs):
    rows, columns = q.shape
    spec = pltpu.PrefetchScalarGridSpec(
        num_scalar_prefetch=1,
        grid=(1,),
        in_specs=[
            pl.BlockSpec(q.shape, lambda i, at: (0, 0)),
            pl.BlockSpec(kv.shape, lambda i, at: (0, 0, 0)),
            pl.BlockSpec((2, rows, 128), lambda i, at: (0, at[0], 0)),
            pl.BlockSpec(wo.shape, lambda i, at: (0, 0)),
        ],
        out_specs=[pl.BlockSpec((pairs, rows, columns), lambda i, at: (0, 0, 0))] * 2,
    )
    return pl.pallas_call(
        latent_kernel,
        grid_spec=spec,
        out_shape=share_shapes(pairs, rows, columns),
        compiler_params=params(24),
        name="latent_attention",
    )(where, q, kv, words, wo)


def exchange(value, axis):
    return lax.all_to_all(value, axis, 0, 0, tiled=True)


def to_partner(value):
    count = lax.axis_size("head")
    return lax.ppermute(value, "head", [(i, i ^ 1) for i in range(count)])


def along_chips(value, distance):
    count = lax.axis_size("head")
    return lax.ppermute(
        value, "head", [(i, (i + 2 * distance) % count) for i in range(count)]
    )


def head_sum(where, own, theirs):
    kept, *sent = chip_sum(where, own, to_partner(theirs))
    return [kept] + [along_chips(value, d) for d, value in enumerate(sent, 1)]


def spread(pieces, seq_index):
    count = len(pieces)
    pair = pieces[count - 1]
    for k in range(count - 1):
        got = lax.ppermute(pieces[k], "seq", [(2 * count - 1, 2 * k + 1)])
        pair = jnp.where(seq_index == 2 * k + 1, got, pair)
    return pair


def pass_on(pair, seq_index, seq_count):
    passed = lax.ppermute(pair[0], "seq", [(k + 1, k) for k in range(0, seq_count, 2)])
    return jnp.where(seq_index % 2 == 0, passed, pair[1])


def per_device(
    context,
    wq_cross,
    wk_cross,
    wv_cross,
    wo_cross,
    wq_latent,
    wk_latent,
    wv_latent,
    wo_latent,
    cross_keep,
    latent_keep,
    residual_keep,
):
    seq_count = lax.axis_size("seq")
    head_count = lax.axis_size("head")
    root = seq_count - 1
    seq_index = lax.axis_index("seq").astype(jnp.int32)
    head_index = lax.axis_index("head").astype(jnp.int32)
    where = jnp.stack([seq_index, head_index])

    chunks = exchange(query_chunks(where, context, wq_cross, seq_count), "seq")
    keys, values = keys_values(context, wk_cross, wv_cross)
    rows, columns = chunks.shape[1:]
    held, keys = lax.optimization_barrier((context, keys))
    held = lax.dynamic_slice_in_dim(held, head_index * columns, columns, 1)
    held = held.reshape(seq_count // 2, 2, rows, columns)
    pieces = [held[k] for k in range(seq_count // 2)]
    own_queries, keys, values, *pieces = lax.optimization_barrier(
        (chunks[root], keys, values, *pieces)
    )
    queries = exchange(
        jnp.broadcast_to(own_queries[None], (seq_count, *own_queries.shape)), "seq"
    )
    queries, *pieces = lax.optimization_barrier((queries, *pieces))
    pair = spread(pieces, seq_index)
    parts = cross_attention(where, queries, keys, values, cross_keep, root)
    pair, parts = lax.optimization_barrier((pair, parts))
    parts = exchange(parts, "seq")
    inputs = pass_on(pair, seq_index, seq_count)
    parts, inputs = lax.optimization_barrier((parts, inputs))
    pairs = head_count // 2
    own, theirs = combine(where, parts, wo_cross, pairs)
    latents = residual(where, head_sum(where, own, theirs), inputs, residual_keep, 0)
    near = jnp.stack([latents] + [along_chips(latents, d) for d in range(1, pairs)])
    far = to_partner(near)
    q, kv = latent_qkv(where, near, far, wq_latent, wk_latent, wv_latent, seq_count)
    kv = exchange(kv, "seq")
    own, theirs = latent_attention(where, q, kv, latent_keep, wo_latent, pairs)
    return residual(where, head_sum(where, own, theirs), latents, residual_keep, 1)


def solution(mesh):
    in_specs = (
        P("seq", None),
        P(None, "head"),
        P(None, "head"),
        P(None, "head"),
        P("head", None),
        P(None, "head"),
        P(None, "head"),
        P(None, "head"),
        P("head", None),
        P("head", None, "seq"),
        P("head", None, None),
        P(),
    )
    out_specs = P("seq", "head")

    return jax.shard_map(
        per_device, mesh=mesh, in_specs=in_specs, out_specs=out_specs, check_vma=False
    )
```

profile of v0, /device:TPU:1, one launch (start us, length us, event | category | flops | bytes accessed | tf_op | source)
XLA Modules:
  0.0 171.9 jit_solution(11454630023674989295)
XLA Ops:
  0.1 3.9 %queries.1 = bf16[16,128,256]{2,1,0:T(8,128)(2,1)} custom-call(s32[2]{0:T(128)S(1)} %pad_add_fusion.refs_0_.where_ref, bf16[2048,2048]{1,0:T(8,128)(2,1)} %x_ref.1, bf16[2048,256]{1,0:T(8,128)(2,1)} %refs_2_.1), custom_call_target="tpu_custom_call" | custom-call | tf_op jit(solution)/shard_map/queries/pallas_call | solution.py:57
  4.0 11.5 %all-to-all-start = ((bf16[16,128,256]{2,1,0:T(8,128)(2,1)}), bf16[16,128,256]{2,1,0:T(8,128)(2,1)S(1)}, u32[]{:S(2)}, u32[]{:S(2)}) async-start(bf16[16,128,256]{2,1,0:T(8,128)(2,1)} %queries.1), calls=%async_computation | async-start | bytes 2097152 | tf_op jit(solution)/shard_map/all_to_all | solution.py:469
  15.5 8.5 %keys_values.1 = (bf16[2048,256]{1,0:T(8,128)(2,1)S(1)}, bf16[2048,256]{1,0:T(8,128)(2,1)}) custom-call(bf16[2048,2048]{1,0:T(8,128)(2,1)} %x_ref.1, bf16[2048,256]{1,0:T(8,128)(2,1)} %wk_ref.2, bf16[2048,256]{1,0:T(8,128)(2,1)} %wv_ref.2), custom_call_target="tpu_custom_call" | custom-call | tf_op jit(solution)/shard_map/keys_values/pallas_call | solution.py:77
  25.0 1.4 fusion
  26.4 5.2 %all-to-all-done = bf16[16,128,256]{2,1,0:T(8,128)(2,1)S(1)} async-done(((bf16[16,128,256]{2,1,0:T(8,128)(2,1)}), bf16[16,128,256]{2,1,0:T(8,128)(2,1)S(1)}, u32[]{:S(2)}, u32[]{:S(2)}) %all-to-all-start) | async-done | bytes 1048608 | tf_op jit(solution)/shard_map/all_to_all | solution.py:469
  31.7 20.1 %all_to_all.20.refs_1_ = bf16[16,128,256]{2,1,0:T(8,128)(2,1)S(1)} all-to-all(bf16[16,128,256]{2,1,0:T(8,128)(2,1)S(1)} %broadcast_in_dim.2), channel_id=1, replica_groups=mesh['seq'=16,'head'=8] {'seq'}, dimensions={0} | all-to-all | bytes 2097152 | tf_op jit(solution)/shard_map/all_to_all | solution.py:469
  56.5 16.8 %cross_attention.1 = bf16[16,272,128]{2,1,0:T(8,128)(2,1)} custom-call(s32[2]{0:T(128)S(1)} %pad_add_fusion.refs_0_.where_ref, bf16[16,128,256]{2,1,0:T(8,128)(2,1)S(1)} %all_to_all.20.refs_1_, bf16[2048,256]{1,0:T(8,128)(2,1)} %copy-done.7, bf16[2048,256]{1,0:T(8,128)(2,1)} %get-tuple-element.70.refs_3_, s32[2,2048,256]{2,1,0:T(8,128)} %refs_4_.1), custom_call_target="tpu_custom_call" | custom-call | flops 4294967296 | bytes 4194304 | tf_op jit(solution)/shard_map/cross_attention/pallas_call | solution.py:232
  73.5 7.0 %all-to-all-start.2 = ((bf16[16,272,128]{2,1,0:T(8,128)(2,1)}), bf16[16,272,128]{2,1,0:T(8,128)(2,1)S(1)}, u32[]{:S(2)}, u32[]{:S(2)}) async-start(bf16[16,272,128]{2,1,0:T(8,128)(2,1)} %cross_attention.1), calls=%async_computation.2 | async-start | bytes 2228224 | tf_op jit(solution)/shard_map/all_to_all | solution.py:469
  80.5 1.4 collective-permute-start.7
  81.9 9.7 %collective-permute-done.7 = bf16[128,256]{1,0:T(8,128)(2,1)S(1)} collective-permute-done((bf16[128,256]{1,0:T(8,128)(2,1)S(1)}, bf16[128,256]{1,0:T(8,128)(2,1)S(1)}, u32[]{:S(2)}, u32[]{:S(2)}) %collective-permute-start.7) | collective-permute-done | bytes 65568 | tf_op jit(solution)/shard_map/ppermute | solution.py:499
  91.7 2.5 %all-to-all-done.2.parts_ref = bf16[16,272,128]{2,1,0:T(8,128)(2,1)S(1)} async-done(((bf16[16,272,128]{2,1,0:T(8,128)(2,1)}), bf16[16,272,128]{2,1,0:T(8,128)(2,1)S(1)}, u32[]{:S(2)}, u32[]{:S(2)}) %all-to-all-start.2) | async-done | bytes 1114144 | tf_op jit(solution)/shard_map/all_to_all | solution.py:469
  94.2 1.2 copy-done.2
  95.4 1.7 combine.1
  97.2 5.9 %collective-permute-start.8 = (bf16[4,128,256]{2,1,0:T(8,128)(2,1)S(1)}, bf16[4,128,256]{2,1,0:T(8,128)(2,1)S(1)}, u32[]{:S(2)}, u32[]{:S(2)}) collective-permute-start(bf16[4,128,256]{2,1,0:T(8,128)(2,1)S(1)} %get-tuple-element.75), channel_id=1, source_target_pairs={{0,1},{1,0},{2,3},{3,2},{4,5},{5,4},{6,7},{7,6},{8,9},{9,8},{10,11... | collective-permute-start | bytes 786440 | tf_op jit(solution)/shard_map/ppermute | solution.py:474
  103.0 1.2 collective-permute-done.8.got_ref
  104.8 1.4 collective-permute-start.9
  106.2 2.6 %collective-permute-start.10 = (bf16[128,256]{1,0:T(8,128)(2,1)S(1)}, bf16[128,256]{1,0:T(8,128)(2,1)S(1)}, u32[]{:S(2)}, u32[]{:S(2)}) collective-permute-start(bf16[128,256]{1,0:T(8,128)(2,1)S(1)} %get-tuple-element.78), channel_id=1, source_target_pairs={{0,4},{1,5},{2,6},{3,7},{4,0},{5,1},{6,2},{7,3},{8,12},{9,13},{10,... | collective-permute-start | bytes 196616 | tf_op jit(solution)/shard_map/ppermute | solution.py:479
  109.9 1.9 %collective-permute-done.10.refs_2_ = bf16[128,256]{1,0:T(8,128)(2,1)S(1)} collective-permute-done((bf16[128,256]{1,0:T(8,128)(2,1)S(1)}, bf16[128,256]{1,0:T(8,128)(2,1)S(1)}, u32[]{:S(2)}, u32[]{:S(2)}) %collective-permute-start.10) | collective-permute-done | bytes 65568 | tf_op jit(solution)/shard_map/ppermute | solution.py:479
  112.8 2.1 %collective-permute-start.14 = (bf16[128,256]{1,0:T(8,128)(2,1)S(1)}, bf16[128,256]{1,0:T(8,128)(2,1)S(1)}, u32[]{:S(2)}, u32[]{:S(2)}) collective-permute-start(bf16[128,256]{1,0:T(8,128)(2,1)S(1)} %residual.2.refs_4_), channel_id=1, source_target_pairs={{0,6},{1,7},{2,0},{3,1},{4,2},{5,3},{6,4},{7,5},{8,14},{9,15},{10,... | collective-permute-start | bytes 196616 | tf_op jit(solution)/shard_map/ppermute | solution.py:479
  115.5 1.2 collective-permute-done.14
  116.8 2.8 %collective-permute-done.13 = bf16[128,256]{1,0:T(8,128)(2,1)S(1)} collective-permute-done((bf16[128,256]{1,0:T(8,128)(2,1)S(1)}, bf16[128,256]{1,0:T(8,128)(2,1)S(1)}, u32[]{:S(2)}, u32[]{:S(2)}) %collective-permute-start.13) | collective-permute-done | bytes 65568 | tf_op jit(solution)/shard_map/ppermute | solution.py:479
  119.9 3.6 %collective-permute-start.15 = (bf16[4,128,256]{2,1,0:T(8,128)(2,1)S(1)}, bf16[4,128,256]{2,1,0:T(8,128)(2,1)S(1)}, u32[]{:S(2)}, u32[]{:S(2)}) collective-permute-start(bf16[4,128,256]{2,1,0:T(8,128)(2,1)S(1)} %pad_maximum_fusion.near_ref), channel_id=1, source_target_pairs={{0,1},{1,0},{2,3},{3,2},{4,5},{5,4},{6,7},{7,6},{8,9},{9,8},{10,11... | collective-permute-start | bytes 786440 | tf_op jit(solution)/shard_map/ppermute | solution.py:474
  123.5 1.2 collective-permute-done.15.far_ref
  124.7 1.3 latent_qkv.1
  126.0 31.9 %all_to_all.21.kv_ref = bf16[16,128,512]{2,1,0:T(8,128)(2,1)S(1)} all-to-all(bf16[16,128,512]{2,1,0:T(8,128)(2,1)S(1)} %get-tuple-element.82), channel_id=1, replica_groups=mesh['seq'=16,'head'=8] {'seq'}, dimensions={0} | all-to-all | bytes 4194304 | tf_op jit(solution)/shard_map/all_to_all | solution.py:469
  158.0 2.8 %latent_attention.1 = (f32[4,128,256]{2,1,0:T(8,128)S(1)}, bf16[4,128,256]{2,1,0:T(8,128)(2,1)S(1)}) custom-call(s32[2]{0:T(128)S(1)} %pad_add_fusion.refs_0_.where_ref, bf16[128,256]{1,0:T(8,128)(2,1)S(1)} %get-tuple-element.81.q_ref, bf16[16,128,512]{2,1,0:T(8,128)(2,1)S(1)} %all_to_all.21.kv_ref, s32[2,2048,128]{2,1,0:T(8,128)S(1)} %copy-done.1, ...), custom_call_target="tpu_custom_call" | custom-call | tf_op jit(solution)/shard_map/latent_attention/pallas_call | solution.py:459
  160.8 1.8 %collective-permute-start.16 = (bf16[4,128,256]{2,1,0:T(8,128)(2,1)S(1)}, bf16[4,128,256]{2,1,0:T(8,128)(2,1)S(1)}, u32[]{:S(2)}, u32[]{:S(2)}) collective-permute-start(bf16[4,128,256]{2,1,0:T(8,128)(2,1)S(1)} %get-tuple-element.84), channel_id=1, source_target_pairs={{0,1},{1,0},{2,3},{3,2},{4,5},{5,4},{6,7},{7,6},{8,9},{9,8},{10,11... | collective-permute-start | bytes 786440 | tf_op jit(solution)/shard_map/ppermute | solution.py:474
  162.7 1.2 collective-permute-done.16.got_ref
  164.5 1.7 %collective-permute-start.18 = (bf16[128,256]{1,0:T(8,128)(2,1)S(1)}, bf16[128,256]{1,0:T(8,128)(2,1)S(1)}, u32[]{:S(2)}, u32[]{:S(2)}) collective-permute-start(bf16[128,256]{1,0:T(8,128)(2,1)S(1)} %get-tuple-element.87), channel_id=1, source_target_pairs={{0,4},{1,5},{2,6},{3,7},{4,0},{5,1},{6,2},{7,3},{8,12},{9,13},{10,... | collective-permute-start | bytes 196616 | tf_op jit(solution)/shard_map/ppermute | solution.py:479
  166.3 1.6 collective-permute-start.19
  167.9 2.7 %collective-permute-done.17.refs_1_ = bf16[128,256]{1,0:T(8,128)(2,1)S(1)} collective-permute-done((bf16[128,256]{1,0:T(8,128)(2,1)S(1)}, bf16[128,256]{1,0:T(8,128)(2,1)S(1)}, u32[]{:S(2)}, u32[]{:S(2)}) %collective-permute-start.17) | collective-permute-done | bytes 65568 | tf_op jit(solution)/shard_map/ppermute | solution.py:479
  170.7 1.2 residual.3
  (48 shorter events, 10.5 us)
Async XLA Ops:
  4.0 27.6 %all-to-all-start = ((bf16[16,128,256]{2,1,0:T(8,128)(2,1)}), bf16[16,128,256]{2,1,0:T(8,128)(2,1)S(1)}, u32[]{:S(2)}, u32[]{:S(2)}) async-start(bf16[16,128,256]{2,1,0:T(8,128)(2,1)} %queries.1), calls=%async_computation | async-start | bytes 2097152 | tf_op jit(solution)/shard_map/all_to_all | solution.py:469
  24.0 1.0 copy-start.7
  51.8 3.4 %collective-permute-start = (bf16[2,128,256]{2,1,0:T(8,128)(2,1)S(1)}, bf16[2,128,256]{2,1,0:T(8,128)(2,1)S(1)}, u32[]{:S(2)}, u32[]{:S(2)}) collective-permute-start(bf16[2,128,256]{2,1,0:T(8,128)(2,1)S(1)} %bitcast.28), channel_id=1, source_target_pairs={{120,104},{121,105},{122,106},{123,107},{124,108},{125,109},{126,1... | collective-permute-start | bytes 393224 | tf_op jit(solution)/shard_map/ppermute | solution.py:493
  52.4 3.4 %collective-permute-start.1 = (bf16[2,128,256]{2,1,0:T(8,128)(2,1)S(1)}, bf16[2,128,256]{2,1,0:T(8,128)(2,1)S(1)}, u32[]{:S(2)}, u32[]{:S(2)}) collective-permute-start(bf16[2,128,256]{2,1,0:T(8,128)(2,1)S(1)} %bitcast.27), channel_id=1, source_target_pairs={{120,88},{121,89},{122,90},{123,91},{124,92},{125,93},{126,94},{12... | collective-permute-start | bytes 393224 | tf_op jit(solution)/shard_map/ppermute | solution.py:493
  53.1 20.2 %collective-permute-start.2 = (bf16[2,128,256]{2,1,0:T(8,128)(2,1)S(1)}, bf16[2,128,256]{2,1,0:T(8,128)(2,1)S(1)}, u32[]{:S(2)}, u32[]{:S(2)}) collective-permute-start(bf16[2,128,256]{2,1,0:T(8,128)(2,1)S(1)} %bitcast.26), channel_id=1, source_target_pairs={{120,72},{121,73},{122,74},{123,75},{124,76},{125,77},{126,78},{12... | collective-permute-start | bytes 393224 | tf_op jit(solution)/shard_map/ppermute | solution.py:493
  53.8 19.6 %collective-permute-start.3 = (bf16[2,128,256]{2,1,0:T(8,128)(2,1)S(1)}, bf16[2,128,256]{2,1,0:T(8,128)(2,1)S(1)}, u32[]{:S(2)}, u32[]{:S(2)}) collective-permute-start(bf16[2,128,256]{2,1,0:T(8,128)(2,1)S(1)} %bitcast.25), channel_id=1, source_target_pairs={{120,56},{121,57},{122,58},{123,59},{124,60},{125,61},{126,62},{12... | collective-permute-start | bytes 393224 | tf_op jit(solution)/shard_map/ppermute | solution.py:493
  54.5 18.9 %collective-permute-start.4 = (bf16[2,128,256]{2,1,0:T(8,128)(2,1)S(1)}, bf16[2,128,256]{2,1,0:T(8,128)(2,1)S(1)}, u32[]{:S(2)}, u32[]{:S(2)}) collective-permute-start(bf16[2,128,256]{2,1,0:T(8,128)(2,1)S(1)} %bitcast.24), channel_id=1, source_target_pairs={{120,40},{121,41},{122,42},{123,43},{124,44},{125,45},{126,46},{12... | collective-permute-start | bytes 393224 | tf_op jit(solution)/shard_map/ppermute | solution.py:493
  55.2 18.2 %collective-permute-start.5 = (bf16[2,128,256]{2,1,0:T(8,128)(2,1)S(1)}, bf16[2,128,256]{2,1,0:T(8,128)(2,1)S(1)}, u32[]{:S(2)}, u32[]{:S(2)}) collective-permute-start(bf16[2,128,256]{2,1,0:T(8,128)(2,1)S(1)} %bitcast.23), channel_id=1, source_target_pairs={{120,24},{121,25},{122,26},{123,27},{124,28},{125,29},{126,30},{12... | collective-permute-start | bytes 393224 | tf_op jit(solution)/shard_map/ppermute | solution.py:493
  55.9 17.5 %collective-permute-start.6 = (bf16[2,128,256]{2,1,0:T(8,128)(2,1)S(1)}, bf16[2,128,256]{2,1,0:T(8,128)(2,1)S(1)}, u32[]{:S(2)}, u32[]{:S(2)}) collective-permute-start(bf16[2,128,256]{2,1,0:T(8,128)(2,1)S(1)} %bitcast.22), channel_id=1, source_target_pairs={{120,8},{121,9},{122,10},{123,11},{124,12},{125,13},{126,14},{127,... | collective-permute-start | bytes 393224 | tf_op jit(solution)/shard_map/ppermute | solution.py:493
  73.5 20.7 %all-to-all-start.2 = ((bf16[16,272,128]{2,1,0:T(8,128)(2,1)}), bf16[16,272,128]{2,1,0:T(8,128)(2,1)S(1)}, u32[]{:S(2)}, u32[]{:S(2)}) async-start(bf16[16,272,128]{2,1,0:T(8,128)(2,1)} %cross_attention.1), calls=%async_computation.2 | async-start | bytes 2228224 | tf_op jit(solution)/shard_map/all_to_all | solution.py:469
  80.5 31.7 %copy-start = (s32[2,2048,128]{2,1,0:T(8,128)S(1)}, s32[2,2048,128]{2,1,0:T(8,128)}, u32[]{:S(2)}) copy-start(s32[2,2048,128]{2,1,0:T(8,128)} %refs_5_.3) | copy-start | bytes 6291460
  80.5 11.1 %collective-permute-start.7 = (bf16[128,256]{1,0:T(8,128)(2,1)S(1)}, bf16[128,256]{1,0:T(8,128)(2,1)S(1)}, u32[]{:S(2)}, u32[]{:S(2)}) collective-permute-start(bf16[128,256]{1,0:T(8,128)(2,1)S(1)} %slice_bitcast_fusion.1), channel_id=1, source_target_pairs={{8,0},{24,16},{40,32},{56,48},{72,64},{88,80},{104,96},{120,112},{... | collective-permute-start | bytes 196616 | tf_op jit(solution)/shard_map/ppermute | solution.py:499
  94.2 1.2 copy-start.2
  97.1 27.6 %copy-start.3 = (bf16[2048,256]{1,0:T(8,128)(2,1)S(1)}, bf16[2048,256]{1,0:T(8,128)(2,1)}, u32[]{:S(2)}) copy-start(bf16[2048,256]{1,0:T(8,128)(2,1)} %wq_ref.1) | copy-start | bytes 3145732
  97.1 27.6 %copy-start.4 = (bf16[2048,256]{1,0:T(8,128)(2,1)S(1)}, bf16[2048,256]{1,0:T(8,128)(2,1)}, u32[]{:S(2)}) copy-start(bf16[2048,256]{1,0:T(8,128)(2,1)} %wk_ref.3) | copy-start | bytes 3145732
  97.1 27.6 %copy-start.5 = (bf16[2048,256]{1,0:T(8,128)(2,1)S(1)}, bf16[2048,256]{1,0:T(8,128)(2,1)}, u32[]{:S(2)}) copy-start(bf16[2048,256]{1,0:T(8,128)(2,1)} %wv_ref.3) | copy-start | bytes 3145732
  97.2 7.0 %collective-permute-start.8 = (bf16[4,128,256]{2,1,0:T(8,128)(2,1)S(1)}, bf16[4,128,256]{2,1,0:T(8,128)(2,1)S(1)}, u32[]{:S(2)}, u32[]{:S(2)}) collective-permute-start(bf16[4,128,256]{2,1,0:T(8,128)(2,1)S(1)} %get-tuple-element.75), channel_id=1, source_target_pairs={{0,1},{1,0},{2,3},{3,2},{4,5},{5,4},{6,7},{7,6},{8,9},{9,8},{10,11... | collective-permute-start | bytes 786440 | tf_op jit(solution)/shard_map/ppermute | solution.py:474
  104.8 5.1 %collective-permute-start.9 = (bf16[128,256]{1,0:T(8,128)(2,1)S(1)}, bf16[128,256]{1,0:T(8,128)(2,1)S(1)}, u32[]{:S(2)}, u32[]{:S(2)}) collective-permute-start(bf16[128,256]{1,0:T(8,128)(2,1)S(1)} %get-tuple-element.77), channel_id=1, source_target_pairs={{0,2},{1,3},{2,4},{3,5},{4,6},{5,7},{6,0},{7,1},{8,10},{9,11},{10,... | collective-permute-start | bytes 196616 | tf_op jit(solution)/shard_map/ppermute | solution.py:479
  106.2 5.5 %collective-permute-start.10 = (bf16[128,256]{1,0:T(8,128)(2,1)S(1)}, bf16[128,256]{1,0:T(8,128)(2,1)S(1)}, u32[]{:S(2)}, u32[]{:S(2)}) collective-permute-start(bf16[128,256]{1,0:T(8,128)(2,1)S(1)} %get-tuple-element.78), channel_id=1, source_target_pairs={{0,4},{1,5},{2,6},{3,7},{4,0},{5,1},{6,2},{7,3},{8,12},{9,13},{10,... | collective-permute-start | bytes 196616 | tf_op jit(solution)/shard_map/ppermute | solution.py:479
  108.8 3.4 %collective-permute-start.11 = (bf16[128,256]{1,0:T(8,128)(2,1)S(1)}, bf16[128,256]{1,0:T(8,128)(2,1)S(1)}, u32[]{:S(2)}, u32[]{:S(2)}) collective-permute-start(bf16[128,256]{1,0:T(8,128)(2,1)S(1)} %get-tuple-element.79), channel_id=1, source_target_pairs={{0,6},{1,7},{2,0},{3,1},{4,2},{5,3},{6,4},{7,5},{8,14},{9,15},{10,... | collective-permute-start | bytes 196616 | tf_op jit(solution)/shard_map/ppermute | solution.py:479
  112.8 4.0 %collective-permute-start.14 = (bf16[128,256]{1,0:T(8,128)(2,1)S(1)}, bf16[128,256]{1,0:T(8,128)(2,1)S(1)}, u32[]{:S(2)}, u32[]{:S(2)}) collective-permute-start(bf16[128,256]{1,0:T(8,128)(2,1)S(1)} %residual.2.refs_4_), channel_id=1, source_target_pairs={{0,6},{1,7},{2,0},{3,1},{4,2},{5,3},{6,4},{7,5},{8,14},{9,15},{10,... | collective-permute-start | bytes 196616 | tf_op jit(solution)/shard_map/ppermute | solution.py:479
  114.9 4.7 %collective-permute-start.13 = (bf16[128,256]{1,0:T(8,128)(2,1)S(1)}, bf16[128,256]{1,0:T(8,128)(2,1)S(1)}, u32[]{:S(2)}, u32[]{:S(2)}) collective-permute-start(bf16[128,256]{1,0:T(8,128)(2,1)S(1)} %residual.2.refs_4_), channel_id=1, source_target_pairs={{0,4},{1,5},{2,6},{3,7},{4,0},{5,1},{6,2},{7,3},{8,12},{9,13},{10,... | collective-permute-start | bytes 196616 | tf_op jit(solution)/shard_map/ppermute | solution.py:479
  114.9 5.0 %collective-permute-start.12 = (bf16[128,256]{1,0:T(8,128)(2,1)S(1)}, bf16[128,256]{1,0:T(8,128)(2,1)S(1)}, u32[]{:S(2)}, u32[]{:S(2)}) collective-permute-start(bf16[128,256]{1,0:T(8,128)(2,1)S(1)} %residual.2.refs_4_), channel_id=1, source_target_pairs={{0,2},{1,3},{2,4},{3,5},{4,6},{5,7},{6,0},{7,1},{8,10},{9,11},{10,... | collective-permute-start | bytes 196616 | tf_op jit(solution)/shard_map/ppermute | solution.py:479
  119.9 4.8 %collective-permute-start.15 = (bf16[4,128,256]{2,1,0:T(8,128)(2,1)S(1)}, bf16[4,128,256]{2,1,0:T(8,128)(2,1)S(1)}, u32[]{:S(2)}, u32[]{:S(2)}) collective-permute-start(bf16[4,128,256]{2,1,0:T(8,128)(2,1)S(1)} %pad_maximum_fusion.near_ref), channel_id=1, source_target_pairs={{0,1},{1,0},{2,3},{3,2},{4,5},{5,4},{6,7},{7,6},{8,9},{9,8},{10,11... | collective-permute-start | bytes 786440 | tf_op jit(solution)/shard_map/ppermute | solution.py:474
  126.0 32.0 %copy-start.1 = (s32[2,2048,128]{2,1,0:T(8,128)S(1)}, s32[2,2048,128]{2,1,0:T(8,128)}, u32[]{:S(2)}) copy-start(s32[2,2048,128]{2,1,0:T(8,128)} %words_ref.1) | copy-start | bytes 6291460
  126.0 31.9 %copy-start.6 = (bf16[256,2048]{1,0:T(8,128)(2,1)S(1)}, bf16[256,2048]{1,0:T(8,128)(2,1)}, u32[]{:S(2)}) copy-start(bf16[256,2048]{1,0:T(8,128)(2,1)} %wo_ref.3) | copy-start | bytes 3145732
  160.8 3.0 %collective-permute-start.16 = (bf16[4,128,256]{2,1,0:T(8,128)(2,1)S(1)}, bf16[4,128,256]{2,1,0:T(8,128)(2,1)S(1)}, u32[]{:S(2)}, u32[]{:S(2)}) collective-permute-start(bf16[4,128,256]{2,1,0:T(8,128)(2,1)S(1)} %get-tuple-element.84), channel_id=1, source_target_pairs={{0,1},{1,0},{2,3},{3,2},{4,5},{5,4},{6,7},{7,6},{8,9},{9,8},{10,11... | collective-permute-start | bytes 786440 | tf_op jit(solution)/shard_map/ppermute | solution.py:474
  164.4 6.2 %collective-permute-start.17 = (bf16[128,256]{1,0:T(8,128)(2,1)S(1)}, bf16[128,256]{1,0:T(8,128)(2,1)S(1)}, u32[]{:S(2)}, u32[]{:S(2)}) collective-permute-start(bf16[128,256]{1,0:T(8,128)(2,1)S(1)} %get-tuple-element.86), channel_id=1, source_target_pairs={{0,2},{1,3},{2,4},{3,5},{4,6},{5,7},{6,0},{7,1},{8,10},{9,11},{10,... | collective-permute-start | bytes 196616 | tf_op jit(solution)/shard_map/ppermute | solution.py:479
  164.5 6.1 %collective-permute-start.18 = (bf16[128,256]{1,0:T(8,128)(2,1)S(1)}, bf16[128,256]{1,0:T(8,128)(2,1)S(1)}, u32[]{:S(2)}, u32[]{:S(2)}) collective-permute-start(bf16[128,256]{1,0:T(8,128)(2,1)S(1)} %get-tuple-element.87), channel_id=1, source_target_pairs={{0,4},{1,5},{2,6},{3,7},{4,0},{5,1},{6,2},{7,3},{8,12},{9,13},{10,... | collective-permute-start | bytes 196616 | tf_op jit(solution)/shard_map/ppermute | solution.py:479
  166.3 4.4 %collective-permute-start.19 = (bf16[128,256]{1,0:T(8,128)(2,1)S(1)}, bf16[128,256]{1,0:T(8,128)(2,1)S(1)}, u32[]{:S(2)}, u32[]{:S(2)}) collective-permute-start(bf16[128,256]{1,0:T(8,128)(2,1)S(1)} %get-tuple-element.88), channel_id=1, source_target_pairs={{0,6},{1,7},{2,0},{3,1},{4,2},{5,3},{6,4},{7,5},{8,14},{9,15},{10,... | collective-permute-start | bytes 196616 | tf_op jit(solution)/shard_map/ppermute | solution.py:479
where the time goes:
time: 173 us; the launch traced here: 172 us
  blocking collectives  52 us (30%)
  starting transfers between devices  47.2 us (27%)
  Pallas kernels  38.1 us (22%)
  waiting for transfers between devices  30.4 us (18%)
  local copies, waits for them, and re-layouts  3.73 us (2%)
    all_to_all x2, blocking collectives, exchange(): return lax.all_to_all(value, axis, 0, 0, tiled=True)  52 us
    all_to_all x2, starting transfers between devices, exchange(): return lax.all_to_all(value, axis, 0, 0, tiled=True)  18.5 us
    pallas_call x1, Pallas kernels, cross_attention(): pl.pallas_call(lambda *refs: cross_kernel(root, n, count // n, *refs), gr...  16.8 us
    ppermute x3, starting transfers between devices, to_partner(): return lax.ppermute(value, 'head', [(i, i ^ 1) for i in range(count)])  11.3 us
    ppermute x9, starting transfers between devices, along_chips(): lax.ppermute(value, 'head', [(i, (i + 2 * distance) % count) for i in ran...  11.2 us
    ppermute x1, waiting for transfers between devices, pass_on(): lax.ppermute(pair[0], 'seq', [(k + 1, k) for k in range(0, seq_count, 2)])  9.71 us
    ppermute x9, waiting for transfers between devices, along_chips(): lax.ppermute(value, 'head', [(i, (i + 2 * distance) % count) for i in ran...  9.48 us
    pallas_call x1, Pallas kernels, keys_values(): pl.pallas_call(kv_kernel, grid=(tok_rows // block,), in_specs=[pl.BlockSp...  8.49 us
  transfers between devices with their start and end apart: 22, of which 13 were waited for; matrix products, arithmetic and copies ran while one was open for 1% of the time, Pallas kernels for 15%

commit v1 on v0

--- a/solution.py
+++ b/solution.py
@@ -15,6 +15,7 @@
 head_dim = 128
 query_scale = math.log2(math.e) / math.sqrt(head_dim)
 stat_rows = 16
+spread_size = 4
 
 
 def params(limit=48):
@@ -261,7 +262,9 @@
     ]
 
 
-def combine_kernel(where_ref, parts_ref, wo_ref, own_ref, theirs_ref):
+def combine_kernel(where_ref, parts_ref, wo_hbm, own_ref, theirs_ref, wo_ref, sem):
+    fetch = pltpu.make_async_copy(wo_hbm, wo_ref, sem)
+    fetch.start()
     count = parts_ref.shape[0]
     rows = head_dim
     heads = []
@@ -278,6 +281,7 @@
             mixed = part if mixed is None else mixed + part
         heads.append(mixed.astype(bf16))
     attended = jnp.concatenate(heads, axis=1)
+    fetch.wait()
     project_shares(attended, wo_ref, where_ref[1] % 2, own_ref, theirs_ref)
 
 
@@ -288,9 +292,10 @@
         grid=(1,),
         in_specs=[
             pl.BlockSpec(parts.shape, whole),
-            pl.BlockSpec(wo.shape, lambda i, at: (0, 0)),
+            pl.BlockSpec(memory_space=pltpu.HBM),
         ],
         out_specs=[pl.BlockSpec((pairs, head_dim, 256), whole)] * 2,
+        scratch_shapes=[pltpu.VMEM(wo.shape, bf16), pltpu.SemaphoreType.DMA(())],
     )
     return pl.pallas_call(
         combine_kernel,
@@ -298,7 +303,7 @@
         out_shape=share_shapes(pairs, head_dim, 256),
         compiler_params=params(16),
         name="combine",
-    )(where, parts, wo)
+    )(where, parts, pltpu.with_memory_space_constraint(wo, pltpu.HBM))
 
 
 def chip_sum_kernel(where_ref, own_ref, got_ref, kept_ref, *out_refs):
@@ -488,16 +493,23 @@
 
 def spread(pieces, seq_index):
     count = len(pieces)
-    pair = pieces[count - 1]
+    quad = pieces[count - 1]
+    size = quad.shape[0]
     for k in range(count - 1):
-        got = lax.ppermute(pieces[k], "seq", [(2 * count - 1, 2 * k + 1)])
-        pair = jnp.where(seq_index == 2 * k + 1, got, pair)
-    return pair
-
-
-def pass_on(pair, seq_index, seq_count):
-    passed = lax.ppermute(pair[0], "seq", [(k + 1, k) for k in range(0, seq_count, 2)])
-    return jnp.where(seq_index % 2 == 0, passed, pair[1])
+        owner = (k + 1) * size - 1
+        got = lax.ppermute(pieces[k], "seq", [(count * size - 1, owner)])
+        quad = jnp.where(seq_index == owner, got, quad)
+    return quad
+
+
+def pass_on(quad, seq_index, seq_count):
+    size = quad.shape[0]
+    mine = quad[size - 1]
+    for j in range(size - 1):
+        pairs = [(k + size - 1, k + j) for k in range(0, seq_count, size)]
+        got = lax.ppermute(quad[j], "seq", pairs)
+        mine = jnp.where(seq_index % size == j, got, mine)
+    return mine
 
 
 def per_device(
@@ -526,8 +538,8 @@
     rows, columns = chunks.shape[1:]
     held, keys = lax.optimization_barrier((context, keys))
     held = lax.dynamic_slice_in_dim(held, head_index * columns, columns, 1)
-    held = held.reshape(seq_count // 2, 2, rows, columns)
-    pieces = [held[k] for k in range(seq_count // 2)]
+    held = held.reshape(seq_count // spread_size, spread_size, rows, columns)
+    pieces = [held[k] for k in range(seq_count // spread_size)]
     own_queries, keys, values, *pieces = lax.optimization_barrier(
         (chunks[root], keys, values, *pieces)
     )

time: 173 us -> 168 us (0.971)
  blocking collectives: 52 us -> 33.4 us
  waiting for transfers between devices: 30.4 us -> 45.8 us
  starting transfers between devices: 47.2 us -> 44 us
    all_to_all x2 -> x1, blocking collectives: 52 us -> 33.4 us  [exchange(): return lax.all_to_all(value, axis, 0, 0, tiled=True)]
    all_to_all x2 -> x3, waiting for transfers between devices: 7.73 us -> 20.5 us  [exchange(): return lax.all_to_all(value, axis, 0, 0, tiled=True)]
    ppermute x3, starting transfers between devices: 11.3 us -> 6.75 us  [to_partner(): return lax.ppermute(value, 'head', [(i, i ^ 1) for i in range(count)])]
    ppermute x8 -> x6, waiting for transfers between devices: 9.72 us -> 12.4 us  [the longest x3 12.4 us: pass_on(): got = lax.ppermute(quad[j], 'seq', pairs)]
    all_to_all x2 -> x3, starting transfers between devices: 18.5 us -> 20.6 us  [exchange(): return lax.all_to_all(value, axis, 0, 0, tiled=True)]
    ppermute x8 -> x6, starting transfers between devices: 6.09 us -> 5.37 us  [the longest x3 3.35 us: pass_on(): got = lax.ppermute(quad[j], 'seq', pairs)]
  transfers between devices with their start and end apart: 22 -> 21, of which waited for: 13 -> 13; matrix products, arithmetic and copies ran while one was open for 1% -> 2% of each run, Pallas kernels for 15% -> 15%
where the time goes in v1:
time: 168 us
  waiting for transfers between devices  45.8 us (27%)
  starting transfers between devices  44 us (26%)
  Pallas kernels  38.5 us (23%)
  blocking collectives  33.4 us (20%)
  local copies, waits for them, and re-layouts  4.66 us (3%)
    all_to_all x1, blocking collectives, exchange(): return lax.all_to_all(value, axis, 0, 0, tiled=True)  33.4 us
    all_to_all x3, starting transfers between devices, exchange(): return lax.all_to_all(value, axis, 0, 0, tiled=True)  20.6 us
    all_to_all x3, waiting for transfers between devices, exchange(): return lax.all_to_all(value, axis, 0, 0, tiled=True)  20.5 us
    pallas_call x1, Pallas kernels, cross_attention(): pl.pallas_call(lambda *refs: cross_kernel(root, n, count // n, *refs), gr...  16.8 us
    ppermute x3, waiting for transfers between devices, pass_on(): got = lax.ppermute(quad[j], 'seq', pairs)  12.4 us
    ppermute x9, starting transfers between devices, along_chips(): lax.ppermute(value, 'head', [(i, (i + 2 * distance) % count) for i in ran...  11.3 us
    ppermute x9, waiting for transfers between devices, along_chips(): lax.ppermute(value, 'head', [(i, (i + 2 * distance) % count) for i in ran...  9.48 us
    pallas_call x1, Pallas kernels, keys_values(): pl.pallas_call(kv_kernel, grid=(tok_rows // block,), in_specs=[pl.BlockSp...  8.47 us
  transfers between devices with their start and end apart: 21, of which 13 were waited for; matrix products, arithmetic and copies ran while one was open for 2% of the time, Pallas kernels for 15%

profile of v1, /device:TPU:1, one launch (start us, length us, event | category | flops | bytes accessed | tf_op | source)
XLA Modules:
  0.0 167.6 jit_solution(394244848956848560)
XLA Ops:
  0.1 3.9 %queries.1 = bf16[16,128,256]{2,1,0:T(8,128)(2,1)} custom-call(s32[2]{0:T(128)S(1)} %pad_add_fusion.refs_0_.where_ref, bf16[2048,2048]{1,0:T(8,128)(2,1)} %x_ref.1, bf16[2048,256]{1,0:T(8,128)(2,1)} %refs_2_.1), custom_call_target="tpu_custom_call" | custom-call | tf_op jit(solution)/shard_map/queries/pallas_call | solution.py:58
  4.0 11.5 %all-to-all-start = ((bf16[16,128,256]{2,1,0:T(8,128)(2,1)}), bf16[16,128,256]{2,1,0:T(8,128)(2,1)S(1)}, u32[]{:S(2)}, u32[]{:S(2)}) async-start(bf16[16,128,256]{2,1,0:T(8,128)(2,1)} %queries.1), calls=%async_computation | async-start | bytes 2097152 | tf_op jit(solution)/shard_map/all_to_all | solution.py:474
  15.5 8.5 %keys_values.1 = (bf16[2048,256]{1,0:T(8,128)(2,1)S(1)}, bf16[2048,256]{1,0:T(8,128)(2,1)}) custom-call(bf16[2048,2048]{1,0:T(8,128)(2,1)} %x_ref.1, bf16[2048,256]{1,0:T(8,128)(2,1)} %wk_ref.2, bf16[2048,256]{1,0:T(8,128)(2,1)} %wv_ref.2), custom_call_target="tpu_custom_call" | custom-call | tf_op jit(solution)/shard_map/keys_values/pallas_call | solution.py:78
  25.0 1.3 fusion.2
  26.3 5.3 %all-to-all-done = bf16[16,128,256]{2,1,0:T(8,128)(2,1)S(1)} async-done(((bf16[16,128,256]{2,1,0:T(8,128)(2,1)}), bf16[16,128,256]{2,1,0:T(8,128)(2,1)S(1)}, u32[]{:S(2)}, u32[]{:S(2)}) %all-to-all-start) | async-done | bytes 1048608 | tf_op jit(solution)/shard_map/all_to_all | solution.py:474
  32.7 4.2 %all-to-all-start.1 = ((bf16[16,128,256]{2,1,0:T(8,128)(2,1)}), bf16[16,128,256]{2,1,0:T(8,128)(2,1)S(1)}, u32[]{:S(2)}, u32[]{:S(2)}) async-start(bf16[16,128,256]{2,1,0:T(8,128)(2,1)} %broadcast_in_dim.2), calls=%async_computation.1 | async-start | bytes 2097152 | tf_op jit(solution)/shard_map/all_to_all | solution.py:474
  36.9 15.1 %all-to-all-done.1.refs_1_ = bf16[16,128,256]{2,1,0:T(8,128)(2,1)S(1)} async-done(((bf16[16,128,256]{2,1,0:T(8,128)(2,1)}), bf16[16,128,256]{2,1,0:T(8,128)(2,1)S(1)}, u32[]{:S(2)}, u32[]{:S(2)}) %all-to-all-start.1) | async-done | bytes 1048608 | tf_op jit(solution)/shard_map/all_to_all | solution.py:474
  54.1 16.8 %cross_attention.1 = bf16[16,272,128]{2,1,0:T(8,128)(2,1)} custom-call(s32[2]{0:T(128)S(1)} %pad_add_fusion.refs_0_.where_ref, bf16[16,128,256]{2,1,0:T(8,128)(2,1)S(1)} %all-to-all-done.1.refs_1_, bf16[2048,256]{1,0:T(8,128)(2,1)} %copy-done.6, bf16[2048,256]{1,0:T(8,128)(2,1)} %get-tuple-element.54.refs_3_, s32[2,2048,256]{2,1,0:T(8,128)} %refs_4_.1), custom_call_target="tpu_custom_call" | custom-call | flops 4294967296 | bytes 4194304 | tf_op jit(solution)/shard_map/cross_attention/pallas_call | solution.py:233
  71.0 4.9 %all-to-all-start.2 = ((bf16[16,272,128]{2,1,0:T(8,128)(2,1)}), bf16[16,272,128]{2,1,0:T(8,128)(2,1)S(1)}, u32[]{:S(2)}, u32[]{:S(2)}) async-start(bf16[16,272,128]{2,1,0:T(8,128)(2,1)} %cross_attention.1), calls=%async_computation.2 | async-start | bytes 2228224 | tf_op jit(solution)/shard_map/all_to_all | solution.py:474
  77.3 1.3 collective-permute-start.4
  78.6 1.3 collective-permute-start.5
  80.5 12.4 %collective-permute-done.5 = bf16[128,256]{1,0:T(8,128)(2,1)} collective-permute-done((bf16[128,256]{1,0:T(8,128)(2,1)}, bf16[128,256]{1,0:T(8,128)(2,1)}, u32[]{:S(2)}, u32[]{:S(2)}) %collective-permute-start.5) | collective-permute-done | bytes 65568 | tf_op jit(solution)/shard_map/ppermute | solution.py:510
  93.8 2.1 %combine.1 = (f32[4,128,256]{2,1,0:T(8,128)S(1)}, bf16[4,128,256]{2,1,0:T(8,128)(2,1)S(1)}) custom-call(s32[2]{0:T(128)S(1)} %pad_add_fusion.refs_0_.where_ref, bf16[16,272,128]{2,1,0:T(8,128)(2,1)S(1)} %all-to-all-done.2.parts_ref, bf16[256,2048]{1,0:T(8,128)(2,1)} %wo_hbm.1), custom_call_target="tpu_custom_call" | custom-call | tf_op jit(solution)/shard_map/combine/pallas_call | solution.py:300
  96.0 1.3 collective-permute-start.6
  97.3 1.2 collective-permute-done.6.got_ref
  99.0 1.4 collective-permute-start.7
  100.4 2.6 %collective-permute-start.8 = (bf16[128,256]{1,0:T(8,128)(2,1)S(1)}, bf16[128,256]{1,0:T(8,128)(2,1)S(1)}, u32[]{:S(2)}, u32[]{:S(2)}) collective-permute-start(bf16[128,256]{1,0:T(8,128)(2,1)S(1)} %get-tuple-element.62), channel_id=1, source_target_pairs={{0,4},{1,5},{2,6},{3,7},{4,0},{5,1},{6,2},{7,3},{8,12},{9,13},{10,... | collective-permute-start | bytes 196616 | tf_op jit(solution)/shard_map/ppermute | solution.py:484
  104.1 1.9 %collective-permute-done.8.refs_2_ = bf16[128,256]{1,0:T(8,128)(2,1)S(1)} collective-permute-done((bf16[128,256]{1,0:T(8,128)(2,1)S(1)}, bf16[128,256]{1,0:T(8,128)(2,1)S(1)}, u32[]{:S(2)}, u32[]{:S(2)}) %collective-permute-start.8) | collective-permute-done | bytes 65568 | tf_op jit(solution)/shard_map/ppermute | solution.py:484
  107.1 2.1 %collective-permute-start.12 = (bf16[128,256]{1,0:T(8,128)(2,1)S(1)}, bf16[128,256]{1,0:T(8,128)(2,1)S(1)}, u32[]{:S(2)}, u32[]{:S(2)}) collective-permute-start(bf16[128,256]{1,0:T(8,128)(2,1)S(1)} %residual.2.refs_4_), channel_id=1, source_target_pairs={{0,6},{1,7},{2,0},{3,1},{4,2},{5,3},{6,4},{7,5},{8,14},{9,15},{10,... | collective-permute-start | bytes 196616 | tf_op jit(solution)/shard_map/ppermute | solution.py:484
  109.8 1.2 collective-permute-done.12
  111.0 2.8 %collective-permute-done.11 = bf16[128,256]{1,0:T(8,128)(2,1)S(1)} collective-permute-done((bf16[128,256]{1,0:T(8,128)(2,1)S(1)}, bf16[128,256]{1,0:T(8,128)(2,1)S(1)}, u32[]{:S(2)}, u32[]{:S(2)}) %collective-permute-start.11) | collective-permute-done | bytes 65568 | tf_op jit(solution)/shard_map/ppermute | solution.py:484
  114.2 3.6 %collective-permute-start.13 = (bf16[4,128,256]{2,1,0:T(8,128)(2,1)S(1)}, bf16[4,128,256]{2,1,0:T(8,128)(2,1)S(1)}, u32[]{:S(2)}, u32[]{:S(2)}) collective-permute-start(bf16[4,128,256]{2,1,0:T(8,128)(2,1)S(1)} %pad_maximum_fusion.near_ref), channel_id=1, source_target_pairs={{0,1},{1,0},{2,3},{3,2},{4,5},{5,4},{6,7},{7,6},{8,9},{9,8},{10,11... | collective-permute-start | bytes 786440 | tf_op jit(solution)/shard_map/ppermute | solution.py:479
  117.8 1.2 collective-permute-done.13.far_ref
  119.0 1.3 latent_qkv.1
  120.3 33.4 %all_to_all.20.kv_ref = bf16[16,128,512]{2,1,0:T(8,128)(2,1)S(1)} all-to-all(bf16[16,128,512]{2,1,0:T(8,128)(2,1)S(1)} %get-tuple-element.66), channel_id=1, replica_groups=mesh['seq'=16,'head'=8] {'seq'}, dimensions={0} | all-to-all | bytes 4194304 | tf_op jit(solution)/shard_map/all_to_all | solution.py:474
  153.7 2.8 %latent_attention.1 = (f32[4,128,256]{2,1,0:T(8,128)S(1)}, bf16[4,128,256]{2,1,0:T(8,128)(2,1)S(1)}) custom-call(s32[2]{0:T(128)S(1)} %pad_add_fusion.refs_0_.where_ref, bf16[128,256]{1,0:T(8,128)(2,1)S(1)} %get-tuple-element.65.q_ref, bf16[16,128,512]{2,1,0:T(8,128)(2,1)S(1)} %all_to_all.20.kv_ref, s32[2,2048,128]{2,1,0:T(8,128)S(1)} %copy-done.1, ...), custom_call_target="tpu_custom_call" | custom-call | tf_op jit(solution)/shard_map/latent_attention/pallas_call | solution.py:464
  156.6 1.8 %collective-permute-start.14 = (bf16[4,128,256]{2,1,0:T(8,128)(2,1)S(1)}, bf16[4,128,256]{2,1,0:T(8,128)(2,1)S(1)}, u32[]{:S(2)}, u32[]{:S(2)}) collective-permute-start(bf16[4,128,256]{2,1,0:T(8,128)(2,1)S(1)} %get-tuple-element.68), channel_id=1, source_target_pairs={{0,1},{1,0},{2,3},{3,2},{4,5},{5,4},{6,7},{7,6},{8,9},{9,8},{10,11... | collective-permute-start | bytes 786440 | tf_op jit(solution)/shard_map/ppermute | solution.py:479
  158.4 1.2 collective-permute-done.14.got_ref
  160.2 1.7 %collective-permute-start.16 = (bf16[128,256]{1,0:T(8,128)(2,1)S(1)}, bf16[128,256]{1,0:T(8,128)(2,1)S(1)}, u32[]{:S(2)}, u32[]{:S(2)}) collective-permute-start(bf16[128,256]{1,0:T(8,128)(2,1)S(1)} %get-tuple-element.71), channel_id=1, source_target_pairs={{0,4},{1,5},{2,6},{3,7},{4,0},{5,1},{6,2},{7,3},{8,12},{9,13},{10,... | collective-permute-start | bytes 196616 | tf_op jit(solution)/shard_map/ppermute | solution.py:484
  162.0 1.6 collective-permute-start.17
  163.6 2.7 %collective-permute-done.15.refs_1_ = bf16[128,256]{1,0:T(8,128)(2,1)S(1)} collective-permute-done((bf16[128,256]{1,0:T(8,128)(2,1)S(1)}, bf16[128,256]{1,0:T(8,128)(2,1)S(1)}, u32[]{:S(2)}, u32[]{:S(2)}) %collective-permute-start.15) | collective-permute-done | bytes 65568 | tf_op jit(solution)/shard_map/ppermute | solution.py:484
  166.4 1.2 residual.3
  (45 shorter events, 11.7 us)
Async XLA Ops:
  4.0 27.6 %all-to-all-start = ((bf16[16,128,256]{2,1,0:T(8,128)(2,1)}), bf16[16,128,256]{2,1,0:T(8,128)(2,1)S(1)}, u32[]{:S(2)}, u32[]{:S(2)}) async-start(bf16[16,128,256]{2,1,0:T(8,128)(2,1)} %queries.1), calls=%async_computation | async-start | bytes 2097152 | tf_op jit(solution)/shard_map/all_to_all | solution.py:474
  24.0 1.0 copy-start.6
  32.7 19.4 %all-to-all-start.1 = ((bf16[16,128,256]{2,1,0:T(8,128)(2,1)}), bf16[16,128,256]{2,1,0:T(8,128)(2,1)S(1)}, u32[]{:S(2)}, u32[]{:S(2)}) async-start(bf16[16,128,256]{2,1,0:T(8,128)(2,1)} %broadcast_in_dim.2), calls=%async_computation.1 | async-start | bytes 2097152 | tf_op jit(solution)/shard_map/all_to_all | solution.py:474
  52.0 18.9 %collective-permute-start = (bf16[4,128,256]{2,1,0:T(8,128)(2,1)S(1)}, bf16[4,128,256]{2,1,0:T(8,128)(2,1)S(1)}, u32[]{:S(2)}, u32[]{:S(2)}) collective-permute-start(bf16[4,128,256]{2,1,0:T(8,128)(2,1)S(1)} %bitcast.28), channel_id=1, source_target_pairs={{120,88},{121,89},{122,90},{123,91},{124,92},{125,93},{126,94},{12... | collective-permute-start | bytes 786440 | tf_op jit(solution)/shard_map/ppermute | solution.py:500
  52.7 18.2 %collective-permute-start.1 = (bf16[4,128,256]{2,1,0:T(8,128)(2,1)S(1)}, bf16[4,128,256]{2,1,0:T(8,128)(2,1)S(1)}, u32[]{:S(2)}, u32[]{:S(2)}) collective-permute-start(bf16[4,128,256]{2,1,0:T(8,128)(2,1)S(1)} %bitcast.27), channel_id=1, source_target_pairs={{120,56},{121,57},{122,58},{123,59},{124,60},{125,61},{126,62},{12... | collective-permute-start | bytes 786440 | tf_op jit(solution)/shard_map/ppermute | solution.py:500
  53.4 17.5 %collective-permute-start.2 = (bf16[4,128,256]{2,1,0:T(8,128)(2,1)S(1)}, bf16[4,128,256]{2,1,0:T(8,128)(2,1)S(1)}, u32[]{:S(2)}, u32[]{:S(2)}) collective-permute-start(bf16[4,128,256]{2,1,0:T(8,128)(2,1)S(1)} %bitcast.26), channel_id=1, source_target_pairs={{120,24},{121,25},{122,26},{123,27},{124,28},{125,29},{126,30},{12... | collective-permute-start | bytes 786440 | tf_op jit(solution)/shard_map/ppermute | solution.py:500
  71.0 22.8 %all-to-all-start.2 = ((bf16[16,272,128]{2,1,0:T(8,128)(2,1)}), bf16[16,272,128]{2,1,0:T(8,128)(2,1)S(1)}, u32[]{:S(2)}, u32[]{:S(2)}) async-start(bf16[16,272,128]{2,1,0:T(8,128)(2,1)} %cross_attention.1), calls=%async_computation.2 | async-start | bytes 2228224 | tf_op jit(solution)/shard_map/all_to_all | solution.py:474
  75.9 30.6 %copy-start = (s32[2,2048,128]{2,1,0:T(8,128)S(1)}, s32[2,2048,128]{2,1,0:T(8,128)}, u32[]{:S(2)}) copy-start(s32[2,2048,128]{2,1,0:T(8,128)} %refs_5_.3) | copy-start | bytes 6291460
  76.5 3.4 %collective-permute-start.3 = (bf16[128,256]{1,0:T(8,128)(2,1)}, bf16[128,256]{1,0:T(8,128)(2,1)S(1)}, u32[]{:S(2)}, u32[]{:S(2)}) collective-permute-start(bf16[128,256]{1,0:T(8,128)(2,1)} %get-tuple-element.79), channel_id=1, source_target_pairs={{24,16},{56,48},{88,80},{120,112},{25,17},{57,49},{89,81},{121,113... | collective-permute-start | bytes 196616 | tf_op jit(solution)/shard_map/ppermute | solution.py:510
  77.3 2.6 %collective-permute-start.4 = (bf16[128,256]{1,0:T(8,128)(2,1)}, bf16[128,256]{1,0:T(8,128)(2,1)}, u32[]{:S(2)}, u32[]{:S(2)}) collective-permute-start(bf16[128,256]{1,0:T(8,128)(2,1)} %get-tuple-element.78), channel_id=1, source_target_pairs={{24,8},{56,40},{88,72},{120,104},{25,9},{57,41},{89,73},{121,105},... | collective-permute-start | bytes 196616 | tf_op jit(solution)/shard_map/ppermute | solution.py:510
  78.6 14.3 %collective-permute-start.5 = (bf16[128,256]{1,0:T(8,128)(2,1)}, bf16[128,256]{1,0:T(8,128)(2,1)}, u32[]{:S(2)}, u32[]{:S(2)}) collective-permute-start(bf16[128,256]{1,0:T(8,128)(2,1)} %get-tuple-element.77), channel_id=1, source_target_pairs={{24,0},{56,32},{88,64},{120,96},{25,1},{57,33},{89,65},{121,97},{2... | collective-permute-start | bytes 196616 | tf_op jit(solution)/shard_map/ppermute | solution.py:510
  79.9 0.6 copy-start.7
  95.9 23.0 %copy-start.2 = (bf16[2048,256]{1,0:T(8,128)(2,1)S(1)}, bf16[2048,256]{1,0:T(8,128)(2,1)}, u32[]{:S(2)}) copy-start(bf16[2048,256]{1,0:T(8,128)(2,1)} %wq_ref.1) | copy-start | bytes 3145732
  95.9 23.0 %copy-start.3 = (bf16[2048,256]{1,0:T(8,128)(2,1)S(1)}, bf16[2048,256]{1,0:T(8,128)(2,1)}, u32[]{:S(2)}) copy-start(bf16[2048,256]{1,0:T(8,128)(2,1)} %wk_ref.3) | copy-start | bytes 3145732
  95.9 23.0 %copy-start.4 = (bf16[2048,256]{1,0:T(8,128)(2,1)S(1)}, bf16[2048,256]{1,0:T(8,128)(2,1)}, u32[]{:S(2)}) copy-start(bf16[2048,256]{1,0:T(8,128)(2,1)} %wv_ref.3) | copy-start | bytes 3145732
  96.0 2.5 %collective-permute-start.6 = (bf16[4,128,256]{2,1,0:T(8,128)(2,1)S(1)}, bf16[4,128,256]{2,1,0:T(8,128)(2,1)S(1)}, u32[]{:S(2)}, u32[]{:S(2)}) collective-permute-start(bf16[4,128,256]{2,1,0:T(8,128)(2,1)S(1)} %get-tuple-element.59), channel_id=1, source_target_pairs={{0,1},{1,0},{2,3},{3,2},{4,5},{5,4},{6,7},{7,6},{8,9},{9,8},{10,11... | collective-permute-start | bytes 786440 | tf_op jit(solution)/shard_map/ppermute | solution.py:479
  99.0 5.1 %collective-permute-start.7 = (bf16[128,256]{1,0:T(8,128)(2,1)S(1)}, bf16[128,256]{1,0:T(8,128)(2,1)S(1)}, u32[]{:S(2)}, u32[]{:S(2)}) collective-permute-start(bf16[128,256]{1,0:T(8,128)(2,1)S(1)} %get-tuple-element.61), channel_id=1, source_target_pairs={{0,2},{1,3},{2,4},{3,5},{4,6},{5,7},{6,0},{7,1},{8,10},{9,11},{10,... | collective-permute-start | bytes 196616 | tf_op jit(solution)/shard_map/ppermute | solution.py:484
  100.4 5.6 %collective-permute-start.8 = (bf16[128,256]{1,0:T(8,128)(2,1)S(1)}, bf16[128,256]{1,0:T(8,128)(2,1)S(1)}, u32[]{:S(2)}, u32[]{:S(2)}) collective-permute-start(bf16[128,256]{1,0:T(8,128)(2,1)S(1)} %get-tuple-element.62), channel_id=1, source_target_pairs={{0,4},{1,5},{2,6},{3,7},{4,0},{5,1},{6,2},{7,3},{8,12},{9,13},{10,... | collective-permute-start | bytes 196616 | tf_op jit(solution)/shard_map/ppermute | solution.py:484
  103.0 3.4 %collective-permute-start.9 = (bf16[128,256]{1,0:T(8,128)(2,1)S(1)}, bf16[128,256]{1,0:T(8,128)(2,1)S(1)}, u32[]{:S(2)}, u32[]{:S(2)}) collective-permute-start(bf16[128,256]{1,0:T(8,128)(2,1)S(1)} %get-tuple-element.63), channel_id=1, source_target_pairs={{0,6},{1,7},{2,0},{3,1},{4,2},{5,3},{6,4},{7,5},{8,14},{9,15},{10,... | collective-permute-start | bytes 196616 | tf_op jit(solution)/shard_map/ppermute | solution.py:484
  107.1 4.0 %collective-permute-start.12 = (bf16[128,256]{1,0:T(8,128)(2,1)S(1)}, bf16[128,256]{1,0:T(8,128)(2,1)S(1)}, u32[]{:S(2)}, u32[]{:S(2)}) collective-permute-start(bf16[128,256]{1,0:T(8,128)(2,1)S(1)} %residual.2.refs_4_), channel_id=1, source_target_pairs={{0,6},{1,7},{2,0},{3,1},{4,2},{5,3},{6,4},{7,5},{8,14},{9,15},{10,... | collective-permute-start | bytes 196616 | tf_op jit(solution)/shard_map/ppermute | solution.py:484
  109.1 4.7 %collective-permute-start.11 = (bf16[128,256]{1,0:T(8,128)(2,1)S(1)}, bf16[128,256]{1,0:T(8,128)(2,1)S(1)}, u32[]{:S(2)}, u32[]{:S(2)}) collective-permute-start(bf16[128,256]{1,0:T(8,128)(2,1)S(1)} %residual.2.refs_4_), channel_id=1, source_target_pairs={{0,4},{1,5},{2,6},{3,7},{4,0},{5,1},{6,2},{7,3},{8,12},{9,13},{10,... | collective-permute-start | bytes 196616 | tf_op jit(solution)/shard_map/ppermute | solution.py:484
  109.1 5.0 %collective-permute-start.10 = (bf16[128,256]{1,0:T(8,128)(2,1)S(1)}, bf16[128,256]{1,0:T(8,128)(2,1)S(1)}, u32[]{:S(2)}, u32[]{:S(2)}) collective-permute-start(bf16[128,256]{1,0:T(8,128)(2,1)S(1)} %residual.2.refs_4_), channel_id=1, source_target_pairs={{0,2},{1,3},{2,4},{3,5},{4,6},{5,7},{6,0},{7,1},{8,10},{9,11},{10,... | collective-permute-start | bytes 196616 | tf_op jit(solution)/shard_map/ppermute | solution.py:484
  114.2 4.8 %collective-permute-start.13 = (bf16[4,128,256]{2,1,0:T(8,128)(2,1)S(1)}, bf16[4,128,256]{2,1,0:T(8,128)(2,1)S(1)}, u32[]{:S(2)}, u32[]{:S(2)}) collective-permute-start(bf16[4,128,256]{2,1,0:T(8,128)(2,1)S(1)} %pad_maximum_fusion.near_ref), channel_id=1, source_target_pairs={{0,1},{1,0},{2,3},{3,2},{4,5},{5,4},{6,7},{7,6},{8,9},{9,8},{10,11... | collective-permute-start | bytes 786440 | tf_op jit(solution)/shard_map/ppermute | solution.py:479
  120.3 33.4 %copy-start.1 = (s32[2,2048,128]{2,1,0:T(8,128)S(1)}, s32[2,2048,128]{2,1,0:T(8,128)}, u32[]{:S(2)}) copy-start(s32[2,2048,128]{2,1,0:T(8,128)} %words_ref.1) | copy-start | bytes 6291460
  120.3 33.4 %copy-start.5 = (bf16[256,2048]{1,0:T(8,128)(2,1)S(1)}, bf16[256,2048]{1,0:T(8,128)(2,1)}, u32[]{:S(2)}) copy-start(bf16[256,2048]{1,0:T(8,128)(2,1)} %wo_ref.1) | copy-start | bytes 3145732
  156.6 3.0 %collective-permute-start.14 = (bf16[4,128,256]{2,1,0:T(8,128)(2,1)S(1)}, bf16[4,128,256]{2,1,0:T(8,128)(2,1)S(1)}, u32[]{:S(2)}, u32[]{:S(2)}) collective-permute-start(bf16[4,128,256]{2,1,0:T(8,128)(2,1)S(1)} %get-tuple-element.68), channel_id=1, source_target_pairs={{0,1},{1,0},{2,3},{3,2},{4,5},{5,4},{6,7},{7,6},{8,9},{9,8},{10,11... | collective-permute-start | bytes 786440 | tf_op jit(solution)/shard_map/ppermute | solution.py:479
  160.2 6.2 %collective-permute-start.15 = (bf16[128,256]{1,0:T(8,128)(2,1)S(1)}, bf16[128,256]{1,0:T(8,128)(2,1)S(1)}, u32[]{:S(2)}, u32[]{:S(2)}) collective-permute-start(bf16[128,256]{1,0:T(8,128)(2,1)S(1)} %get-tuple-element.70), channel_id=1, source_target_pairs={{0,2},{1,3},{2,4},{3,5},{4,6},{5,7},{6,0},{7,1},{8,10},{9,11},{10,... | collective-permute-start | bytes 196616 | tf_op jit(solution)/shard_map/ppermute | solution.py:484
  160.2 6.1 %collective-permute-start.16 = (bf16[128,256]{1,0:T(8,128)(2,1)S(1)}, bf16[128,256]{1,0:T(8,128)(2,1)S(1)}, u32[]{:S(2)}, u32[]{:S(2)}) collective-permute-start(bf16[128,256]{1,0:T(8,128)(2,1)S(1)} %get-tuple-element.71), channel_id=1, source_target_pairs={{0,4},{1,5},{2,6},{3,7},{4,0},{5,1},{6,2},{7,3},{8,12},{9,13},{10,... | collective-permute-start | bytes 196616 | tf_op jit(solution)/shard_map/ppermute | solution.py:484
  162.0 4.4 %collective-permute-start.17 = (bf16[128,256]{1,0:T(8,128)(2,1)S(1)}, bf16[128,256]{1,0:T(8,128)(2,1)S(1)}, u32[]{:S(2)}, u32[]{:S(2)}) collective-permute-start(bf16[128,256]{1,0:T(8,128)(2,1)S(1)} %get-tuple-element.72), channel_id=1, source_target_pairs={{0,6},{1,7},{2,0},{3,1},{4,2},{5,3},{6,4},{7,5},{8,14},{9,15},{10,... | collective-permute-start | bytes 196616 | tf_op jit(solution)/shard_map/ppermute | solution.py:484

commit v2 on v1

--- a/solution.py
+++ b/solution.py
@@ -486,9 +486,10 @@
     )
 
 
-def head_sum(where, own, theirs):
+def head_sum(where, own, theirs, beside=()):
     kept, *sent = chip_sum(where, own, to_partner(theirs))
-    return [kept] + [along_chips(value, d) for d, value in enumerate(sent, 1)]
+    *sent, beside = lax.optimization_barrier((*sent, list(beside)))
+    return [kept] + [along_chips(value, d) for d, value in enumerate(sent, 1)], beside
 
 
 def spread(pieces, seq_index):
@@ -502,12 +503,12 @@
     return quad
 
 
-def pass_on(quad, seq_index, seq_count):
-    size = quad.shape[0]
-    mine = quad[size - 1]
+def pass_on(slices, seq_index, seq_count):
+    size = len(slices)
+    mine = slices[size - 1]
     for j in range(size - 1):
         pairs = [(k + size - 1, k + j) for k in range(0, seq_count, size)]
-        got = lax.ppermute(quad[j], "seq", pairs)
+        got = lax.ppermute(slices[j], "seq", pairs)
         mine = jnp.where(seq_index % size == j, got, mine)
     return mine
 
@@ -547,21 +548,23 @@
         jnp.broadcast_to(own_queries[None], (seq_count, *own_queries.shape)), "seq"
     )
     queries, *pieces = lax.optimization_barrier((queries, *pieces))
-    pair = spread(pieces, seq_index)
+    quad = spread(pieces, seq_index)
     parts = cross_attention(where, queries, keys, values, cross_keep, root)
-    pair, parts = lax.optimization_barrier((pair, parts))
+    quad, parts = lax.optimization_barrier((quad, parts))
     parts = exchange(parts, "seq")
-    inputs = pass_on(pair, seq_index, seq_count)
-    parts, inputs = lax.optimization_barrier((parts, inputs))
     pairs = head_count // 2
     own, theirs = combine(where, parts, wo_cross, pairs)
-    latents = residual(where, head_sum(where, own, theirs), inputs, residual_keep, 0)
+    slices = [quad[j] for j in range(spread_size)]
+    shares, slices = head_sum(where, own, theirs, slices)
+    inputs = pass_on(slices, seq_index, seq_count)
+    latents = residual(where, shares, inputs, residual_keep, 0)
     near = jnp.stack([latents] + [along_chips(latents, d) for d in range(1, pairs)])
     far = to_partner(near)
     q, kv = latent_qkv(where, near, far, wq_latent, wk_latent, wv_latent, seq_count)
     kv = exchange(kv, "seq")
     own, theirs = latent_attention(where, q, kv, latent_keep, wo_latent, pairs)
-    return residual(where, head_sum(where, own, theirs), latents, residual_keep, 1)
+    shares, _ = head_sum(where, own, theirs)
+    return residual(where, shares, latents, residual_keep, 1)
 
 
 def solution(mesh):

time: 168 us -> 173 us (1.030)
  blocking collectives: 33.4 us -> 55.2 us
  waiting for transfers between devices: 45.8 us -> 31.9 us
  starting transfers between devices: 44 us -> 41.4 us
    all_to_all x1 -> x2, blocking collectives: 33.4 us -> 55.2 us  [exchange(): return lax.all_to_all(value, axis, 0, 0, tiled=True)]
    ppermute x3, waiting for transfers between devices: 12.4 us -> 0.77 us  [pass_on(): got = lax.ppermute(slices[j], 'seq', pairs)]
    all_to_all x3 -> x2, starting transfers between devices: 20.6 us -> 15.7 us  [exchange(): return lax.all_to_all(value, axis, 0, 0, tiled=True)]
    all_to_all x3 -> x2, waiting for transfers between devices: 20.5 us -> 20.5 us  [exchange(): return lax.all_to_all(value, axis, 0, 0, tiled=True)]
  transfers between devices with their start and end apart: 21 -> 20, of which waited for: 13 -> 13; matrix products, arithmetic and copies ran while one was open for 2% -> 2% of each run, Pallas kernels for 15% -> 15%
where the time goes in v2:
time: 173 us; the launch traced here: 172 us
  blocking collectives  55.2 us (32%)
  starting transfers between devices  41.4 us (24%)
  Pallas kernels  38.6 us (22%)
  waiting for transfers between devices  31.9 us (18%)
  local copies, waits for them, and re-layouts  4.02 us (2%)
    all_to_all x2, blocking collectives, exchange(): return lax.all_to_all(value, axis, 0, 0, tiled=True)  55.2 us
    all_to_all x2, waiting for transfers between devices, exchange(): return lax.all_to_all(value, axis, 0, 0, tiled=True)  20.5 us
    pallas_call x1, Pallas kernels, cross_attention(): pl.pallas_call(lambda *refs: cross_kernel(root, n, count // n, *refs), gr...  16.8 us
    all_to_all x2, starting transfers between devices, exchange(): return lax.all_to_all(value, axis, 0, 0, tiled=True)  15.7 us
    ppermute x9, starting transfers between devices, along_chips(): lax.ppermute(value, 'head', [(i, (i + 2 * distance) % count) for i in ran...  11.7 us
    pallas_call x1, Pallas kernels, keys_values(): pl.pallas_call(kv_kernel, grid=(tok_rows // block,), in_specs=[pl.BlockSp...  8.48 us
    ppermute x3, starting transfers between devices, to_partner(): return lax.ppermute(value, 'head', [(i, i ^ 1) for i in range(count)])  8.1 us
    ppermute x9, waiting for transfers between devices, along_chips(): lax.ppermute(value, 'head', [(i, (i + 2 * distance) % count) for i in ran...  7.81 us
  transfers between devices with their start and end apart: 20, of which 13 were waited for; matrix products, arithmetic and copies ran while one was open for 2% of the time, Pallas kernels for 15%

profile of v2, /device:TPU:1, one launch (start us, length us, event | category | flops | bytes accessed | tf_op | source)
XLA Modules:
  0.0 172.3 jit_solution(17702663578054208249)
XLA Ops:
  0.1 3.9 %queries.1 = bf16[16,128,256]{2,1,0:T(8,128)(2,1)} custom-call(s32[2]{0:T(128)S(1)} %pad_add_fusion.refs_0_.where_ref, bf16[2048,2048]{1,0:T(8,128)(2,1)} %x_ref.1, bf16[2048,256]{1,0:T(8,128)(2,1)} %refs_2_.1), custom_call_target="tpu_custom_call" | custom-call | tf_op jit(solution)/shard_map/queries/pallas_call | solution.py:58
  4.0 11.5 %all-to-all-start = ((bf16[16,128,256]{2,1,0:T(8,128)(2,1)}), bf16[16,128,256]{2,1,0:T(8,128)(2,1)S(1)}, u32[]{:S(2)}, u32[]{:S(2)}) async-start(bf16[16,128,256]{2,1,0:T(8,128)(2,1)} %queries.1), calls=%async_computation | async-start | bytes 2097152 | tf_op jit(solution)/shard_map/all_to_all | solution.py:474
  15.5 8.5 %keys_values.1 = (bf16[2048,256]{1,0:T(8,128)(2,1)S(1)}, bf16[2048,256]{1,0:T(8,128)(2,1)}) custom-call(bf16[2048,2048]{1,0:T(8,128)(2,1)} %x_ref.1, bf16[2048,256]{1,0:T(8,128)(2,1)} %wk_ref.2, bf16[2048,256]{1,0:T(8,128)(2,1)} %wv_ref.2), custom_call_target="tpu_custom_call" | custom-call | tf_op jit(solution)/shard_map/keys_values/pallas_call | solution.py:78
  24.0 1.0 copy-done.6
  25.0 1.3 fusion
  26.3 5.3 %all-to-all-done = bf16[16,128,256]{2,1,0:T(8,128)(2,1)S(1)} async-done(((bf16[16,128,256]{2,1,0:T(8,128)(2,1)}), bf16[16,128,256]{2,1,0:T(8,128)(2,1)S(1)}, u32[]{:S(2)}, u32[]{:S(2)}) %all-to-all-start) | async-done | bytes 1048608 | tf_op jit(solution)/shard_map/all_to_all | solution.py:474
  31.6 1.1 broadcast_in_dim.2
  32.7 4.2 %all-to-all-start.1 = ((bf16[16,128,256]{2,1,0:T(8,128)(2,1)}), bf16[16,128,256]{2,1,0:T(8,128)(2,1)S(1)}, u32[]{:S(2)}, u32[]{:S(2)}) async-start(bf16[16,128,256]{2,1,0:T(8,128)(2,1)} %broadcast_in_dim.2), calls=%async_computation.1 | async-start | bytes 2097152 | tf_op jit(solution)/shard_map/all_to_all | solution.py:474
  36.9 15.1 %all-to-all-done.1.refs_1_ = bf16[16,128,256]{2,1,0:T(8,128)(2,1)S(1)} async-done(((bf16[16,128,256]{2,1,0:T(8,128)(2,1)}), bf16[16,128,256]{2,1,0:T(8,128)(2,1)S(1)}, u32[]{:S(2)}, u32[]{:S(2)}) %all-to-all-start.1) | async-done | bytes 1048608 | tf_op jit(solution)/shard_map/all_to_all | solution.py:474
  54.1 16.8 %cross_attention.1 = bf16[16,272,128]{2,1,0:T(8,128)(2,1)} custom-call(s32[2]{0:T(128)S(1)} %pad_add_fusion.refs_0_.where_ref, bf16[16,128,256]{2,1,0:T(8,128)(2,1)S(1)} %all-to-all-done.1.refs_1_, bf16[2048,256]{1,0:T(8,128)(2,1)} %copy-done.6, bf16[2048,256]{1,0:T(8,128)(2,1)} %get-tuple-element.62.refs_3_, s32[2,2048,256]{2,1,0:T(8,128)} %refs_4_.1), custom_call_target="tpu_custom_call" | custom-call | flops 4294967296 | bytes 4194304 | tf_op jit(solution)/shard_map/cross_attention/pallas_call | solution.py:233
  71.0 20.9 %all_to_all.20.parts_ref = bf16[16,272,128]{2,1,0:T(8,128)(2,1)S(1)} all-to-all(bf16[16,272,128]{2,1,0:T(8,128)(2,1)} %cross_attention.1), channel_id=1, replica_groups=mesh['seq'=16,'head'=8] {'seq'}, dimensions={0} | all-to-all | bytes 2228224 | tf_op jit(solution)/shard_map/all_to_all | solution.py:474
  91.9 2.2 %combine.1 = (f32[4,128,256]{2,1,0:T(8,128)S(1)}, bf16[4,128,256]{2,1,0:T(8,128)(2,1)S(1)}) custom-call(s32[2]{0:T(128)S(1)} %pad_add_fusion.refs_0_.where_ref, bf16[16,272,128]{2,1,0:T(8,128)(2,1)S(1)} %all_to_all.20.parts_ref, bf16[256,2048]{1,0:T(8,128)(2,1)} %wo_hbm.1), custom_call_target="tpu_custom_call" | custom-call | tf_op jit(solution)/shard_map/combine/pallas_call | solution.py:300
  94.1 2.9 %collective-permute-start.3 = (bf16[4,128,256]{2,1,0:T(8,128)(2,1)S(1)}, bf16[4,128,256]{2,1,0:T(8,128)(2,1)S(1)}, u32[]{:S(2)}, u32[]{:S(2)}) collective-permute-start(bf16[4,128,256]{2,1,0:T(8,128)(2,1)S(1)} %get-tuple-element.65), channel_id=1, source_target_pairs={{0,1},{1,0},{2,3},{3,2},{4,5},{5,4},{6,7},{7,6},{8,9},{9,8},{10,11... | collective-permute-start | bytes 786440 | tf_op jit(solution)/shard_map/ppermute | solution.py:479
  98.8 1.3 collective-permute-start.7
  100.1 1.3 collective-permute-start.8
  101.4 1.3 collective-permute-start.9
  102.7 1.3 collective-permute-start.4
  104.1 2.6 %collective-permute-start.5 = (bf16[128,256]{1,0:T(8,128)(2,1)S(1)}, bf16[128,256]{1,0:T(8,128)(2,1)S(1)}, u32[]{:S(2)}, u32[]{:S(2)}) collective-permute-start(bf16[128,256]{1,0:T(8,128)(2,1)S(1)} %get-tuple-element.72), channel_id=1, source_target_pairs={{0,4},{1,5},{2,6},{3,7},{4,0},{5,1},{6,2},{7,3},{8,12},{9,13},{10,... | collective-permute-start | bytes 196616 | tf_op jit(solution)/shard_map/ppermute | solution.py:484
  106.7 1.1 collective-permute-start.6
  110.8 2.3 %collective-permute-start.12 = (bf16[128,256]{1,0:T(8,128)(2,1)S(1)}, bf16[128,256]{1,0:T(8,128)(2,1)S(1)}, u32[]{:S(2)}, u32[]{:S(2)}) collective-permute-start(bf16[128,256]{1,0:T(8,128)(2,1)S(1)} %residual.2.refs_4_), channel_id=1, source_target_pairs={{0,6},{1,7},{2,0},{3,1},{4,2},{5,3},{6,4},{7,5},{8,14},{9,15},{10,... | collective-permute-start | bytes 196616 | tf_op jit(solution)/shard_map/ppermute | solution.py:484
  114.4 3.4 %collective-permute-done.11 = bf16[128,256]{1,0:T(8,128)(2,1)S(1)} collective-permute-done((bf16[128,256]{1,0:T(8,128)(2,1)S(1)}, bf16[128,256]{1,0:T(8,128)(2,1)S(1)}, u32[]{:S(2)}, u32[]{:S(2)}) %collective-permute-start.11) | collective-permute-done | bytes 65568 | tf_op jit(solution)/shard_map/ppermute | solution.py:484
  118.3 3.3 %collective-permute-start.13 = (bf16[4,128,256]{2,1,0:T(8,128)(2,1)S(1)}, bf16[4,128,256]{2,1,0:T(8,128)(2,1)S(1)}, u32[]{:S(2)}, u32[]{:S(2)}) collective-permute-start(bf16[4,128,256]{2,1,0:T(8,128)(2,1)S(1)} %pad_maximum_fusion.near_ref), channel_id=1, source_target_pairs={{0,1},{1,0},{2,3},{3,2},{4,5},{5,4},{6,7},{7,6},{8,9},{9,8},{10,11... | collective-permute-start | bytes 786440 | tf_op jit(solution)/shard_map/ppermute | solution.py:479
  121.6 1.2 collective-permute-done.13.far_ref
  122.8 1.3 latent_qkv.1
  124.1 34.2 %all_to_all.21.kv_ref = bf16[16,128,512]{2,1,0:T(8,128)(2,1)S(1)} all-to-all(bf16[16,128,512]{2,1,0:T(8,128)(2,1)S(1)} %get-tuple-element.79), channel_id=1, replica_groups=mesh['seq'=16,'head'=8] {'seq'}, dimensions={0} | all-to-all | bytes 4194304 | tf_op jit(solution)/shard_map/all_to_all | solution.py:474
  158.3 2.8 %latent_attention.1 = (f32[4,128,256]{2,1,0:T(8,128)S(1)}, bf16[4,128,256]{2,1,0:T(8,128)(2,1)S(1)}) custom-call(s32[2]{0:T(128)S(1)} %pad_add_fusion.refs_0_.where_ref, bf16[128,256]{1,0:T(8,128)(2,1)S(1)} %get-tuple-element.78.q_ref, bf16[16,128,512]{2,1,0:T(8,128)(2,1)S(1)} %all_to_all.21.kv_ref, s32[2,2048,128]{2,1,0:T(8,128)S(1)} %copy-done.1, ...), custom_call_target="tpu_custom_call" | custom-call | tf_op jit(solution)/shard_map/latent_attention/pallas_call | solution.py:464
  161.2 1.8 %collective-permute-start.14 = (bf16[4,128,256]{2,1,0:T(8,128)(2,1)S(1)}, bf16[4,128,256]{2,1,0:T(8,128)(2,1)S(1)}, u32[]{:S(2)}, u32[]{:S(2)}) collective-permute-start(bf16[4,128,256]{2,1,0:T(8,128)(2,1)S(1)} %get-tuple-element.81), channel_id=1, source_target_pairs={{0,1},{1,0},{2,3},{3,2},{4,5},{5,4},{6,7},{7,6},{8,9},{9,8},{10,11... | collective-permute-start | bytes 786440 | tf_op jit(solution)/shard_map/ppermute | solution.py:479
  163.0 1.2 collective-permute-done.14.got_ref
  164.9 1.7 %collective-permute-start.16 = (bf16[128,256]{1,0:T(8,128)(2,1)S(1)}, bf16[128,256]{1,0:T(8,128)(2,1)S(1)}, u32[]{:S(2)}, u32[]{:S(2)}) collective-permute-start(bf16[128,256]{1,0:T(8,128)(2,1)S(1)} %get-tuple-element.87), channel_id=1, source_target_pairs={{0,4},{1,5},{2,6},{3,7},{4,0},{5,1},{6,2},{7,3},{8,12},{9,13},{10,... | collective-permute-start | bytes 196616 | tf_op jit(solution)/shard_map/ppermute | solution.py:484
  166.6 1.6 collective-permute-start.17
  168.3 2.7 %collective-permute-done.15.refs_1_ = bf16[128,256]{1,0:T(8,128)(2,1)S(1)} collective-permute-done((bf16[128,256]{1,0:T(8,128)(2,1)S(1)}, bf16[128,256]{1,0:T(8,128)(2,1)S(1)}, u32[]{:S(2)}, u32[]{:S(2)}) %collective-permute-start.15) | collective-permute-done | bytes 65568 | tf_op jit(solution)/shard_map/ppermute | solution.py:484
  171.1 1.2 residual.3
  (42 shorter events, 9.4 us)
Async XLA Ops:
  4.0 27.6 %all-to-all-start = ((bf16[16,128,256]{2,1,0:T(8,128)(2,1)}), bf16[16,128,256]{2,1,0:T(8,128)(2,1)S(1)}, u32[]{:S(2)}, u32[]{:S(2)}) async-start(bf16[16,128,256]{2,1,0:T(8,128)(2,1)} %queries.1), calls=%async_computation | async-start | bytes 2097152 | tf_op jit(solution)/shard_map/all_to_all | solution.py:474
  24.0 1.0 copy-start.6
  32.7 19.4 %all-to-all-start.1 = ((bf16[16,128,256]{2,1,0:T(8,128)(2,1)}), bf16[16,128,256]{2,1,0:T(8,128)(2,1)S(1)}, u32[]{:S(2)}, u32[]{:S(2)}) async-start(bf16[16,128,256]{2,1,0:T(8,128)(2,1)} %broadcast_in_dim.2), calls=%async_computation.1 | async-start | bytes 2097152 | tf_op jit(solution)/shard_map/all_to_all | solution.py:474
  52.0 18.9 %collective-permute-start = (bf16[4,128,256]{2,1,0:T(8,128)(2,1)S(1)}, bf16[4,128,256]{2,1,0:T(8,128)(2,1)S(1)}, u32[]{:S(2)}, u32[]{:S(2)}) collective-permute-start(bf16[4,128,256]{2,1,0:T(8,128)(2,1)S(1)} %bitcast.24), channel_id=1, source_target_pairs={{120,88},{121,89},{122,90},{123,91},{124,92},{125,93},{126,94},{12... | collective-permute-start | bytes 786440 | tf_op jit(solution)/shard_map/ppermute | solution.py:501
  52.7 18.2 %collective-permute-start.1 = (bf16[4,128,256]{2,1,0:T(8,128)(2,1)S(1)}, bf16[4,128,256]{2,1,0:T(8,128)(2,1)S(1)}, u32[]{:S(2)}, u32[]{:S(2)}) collective-permute-start(bf16[4,128,256]{2,1,0:T(8,128)(2,1)S(1)} %bitcast.23), channel_id=1, source_target_pairs={{120,56},{121,57},{122,58},{123,59},{124,60},{125,61},{126,62},{12... | collective-permute-start | bytes 786440 | tf_op jit(solution)/shard_map/ppermute | solution.py:501
  53.4 17.5 %collective-permute-start.2 = (bf16[4,128,256]{2,1,0:T(8,128)(2,1)S(1)}, bf16[4,128,256]{2,1,0:T(8,128)(2,1)S(1)}, u32[]{:S(2)}, u32[]{:S(2)}) collective-permute-start(bf16[4,128,256]{2,1,0:T(8,128)(2,1)S(1)} %bitcast.22), channel_id=1, source_target_pairs={{120,24},{121,25},{122,26},{123,27},{124,28},{125,29},{126,30},{12... | collective-permute-start | bytes 786440 | tf_op jit(solution)/shard_map/ppermute | solution.py:501
  91.9 18.2 %copy-start = (s32[2,2048,128]{2,1,0:T(8,128)S(1)}, s32[2,2048,128]{2,1,0:T(8,128)}, u32[]{:S(2)}) copy-start(s32[2,2048,128]{2,1,0:T(8,128)} %refs_5_.3) | copy-start | bytes 6291460
  94.1 4.1 %collective-permute-start.3 = (bf16[4,128,256]{2,1,0:T(8,128)(2,1)S(1)}, bf16[4,128,256]{2,1,0:T(8,128)(2,1)S(1)}, u32[]{:S(2)}, u32[]{:S(2)}) collective-permute-start(bf16[4,128,256]{2,1,0:T(8,128)(2,1)S(1)} %get-tuple-element.65), channel_id=1, source_target_pairs={{0,1},{1,0},{2,3},{3,2},{4,5},{5,4},{6,7},{7,6},{8,9},{9,8},{10,11... | collective-permute-start | bytes 786440 | tf_op jit(solution)/shard_map/ppermute | solution.py:479
  98.2 24.5 %copy-start.2 = (bf16[2048,256]{1,0:T(8,128)(2,1)S(1)}, bf16[2048,256]{1,0:T(8,128)(2,1)}, u32[]{:S(2)}) copy-start(bf16[2048,256]{1,0:T(8,128)(2,1)} %wq_ref.1) | copy-start | bytes 3145732
  98.8 7.9 %collective-permute-start.7 = (bf16[128,256]{1,0:T(8,128)(2,1)}, bf16[128,256]{1,0:T(8,128)(2,1)}, u32[]{:S(2)}, u32[]{:S(2)}) collective-permute-start(bf16[128,256]{1,0:T(8,128)(2,1)} %get-tuple-element.74), channel_id=1, source_target_pairs={{24,16},{56,48},{88,80},{120,112},{25,17},{57,49},{89,81},{121,113... | collective-permute-start | bytes 196616 | tf_op jit(solution)/shard_map/ppermute | solution.py:511
  100.1 7.7 %collective-permute-start.8 = (bf16[128,256]{1,0:T(8,128)(2,1)}, bf16[128,256]{1,0:T(8,128)(2,1)}, u32[]{:S(2)}, u32[]{:S(2)}) collective-permute-start(bf16[128,256]{1,0:T(8,128)(2,1)} %get-tuple-element.75), channel_id=1, source_target_pairs={{24,8},{56,40},{88,72},{120,104},{25,9},{57,41},{89,73},{121,105},... | collective-permute-start | bytes 196616 | tf_op jit(solution)/shard_map/ppermute | solution.py:511
  101.4 7.2 %collective-permute-start.9 = (bf16[128,256]{1,0:T(8,128)(2,1)}, bf16[128,256]{1,0:T(8,128)(2,1)}, u32[]{:S(2)}, u32[]{:S(2)}) collective-permute-start(bf16[128,256]{1,0:T(8,128)(2,1)} %get-tuple-element.76), channel_id=1, source_target_pairs={{24,0},{56,32},{88,64},{120,96},{25,1},{57,33},{89,65},{121,97},{2... | collective-permute-start | bytes 196616 | tf_op jit(solution)/shard_map/ppermute | solution.py:511
  102.7 20.1 %copy-start.3 = (bf16[2048,256]{1,0:T(8,128)(2,1)S(1)}, bf16[2048,256]{1,0:T(8,128)(2,1)}, u32[]{:S(2)}) copy-start(bf16[2048,256]{1,0:T(8,128)(2,1)} %wk_ref.3) | copy-start | bytes 3145732
  102.7 20.0 %copy-start.4 = (bf16[2048,256]{1,0:T(8,128)(2,1)S(1)}, bf16[2048,256]{1,0:T(8,128)(2,1)}, u32[]{:S(2)}) copy-start(bf16[2048,256]{1,0:T(8,128)(2,1)} %wv_ref.3) | copy-start | bytes 3145732
  102.7 6.7 %collective-permute-start.4 = (bf16[128,256]{1,0:T(8,128)(2,1)S(1)}, bf16[128,256]{1,0:T(8,128)(2,1)S(1)}, u32[]{:S(2)}, u32[]{:S(2)}) collective-permute-start(bf16[128,256]{1,0:T(8,128)(2,1)S(1)} %get-tuple-element.71), channel_id=1, source_target_pairs={{0,2},{1,3},{2,4},{3,5},{4,6},{5,7},{6,0},{7,1},{8,10},{9,11},{10,... | collective-permute-start | bytes 196616 | tf_op jit(solution)/shard_map/ppermute | solution.py:484
  104.1 5.6 %collective-permute-start.5 = (bf16[128,256]{1,0:T(8,128)(2,1)S(1)}, bf16[128,256]{1,0:T(8,128)(2,1)S(1)}, u32[]{:S(2)}, u32[]{:S(2)}) collective-permute-start(bf16[128,256]{1,0:T(8,128)(2,1)S(1)} %get-tuple-element.72), channel_id=1, source_target_pairs={{0,4},{1,5},{2,6},{3,7},{4,0},{5,1},{6,2},{7,3},{8,12},{9,13},{10,... | collective-permute-start | bytes 196616 | tf_op jit(solution)/shard_map/ppermute | solution.py:484
  106.7 3.4 %collective-permute-start.6 = (bf16[128,256]{1,0:T(8,128)(2,1)S(1)}, bf16[128,256]{1,0:T(8,128)(2,1)S(1)}, u32[]{:S(2)}, u32[]{:S(2)}) collective-permute-start(bf16[128,256]{1,0:T(8,128)(2,1)S(1)} %get-tuple-element.73), channel_id=1, source_target_pairs={{0,6},{1,7},{2,0},{3,1},{4,2},{5,3},{6,4},{7,5},{8,14},{9,15},{10,... | collective-permute-start | bytes 196616 | tf_op jit(solution)/shard_map/ppermute | solution.py:484
  110.8 3.7 %collective-permute-start.12 = (bf16[128,256]{1,0:T(8,128)(2,1)S(1)}, bf16[128,256]{1,0:T(8,128)(2,1)S(1)}, u32[]{:S(2)}, u32[]{:S(2)}) collective-permute-start(bf16[128,256]{1,0:T(8,128)(2,1)S(1)} %residual.2.refs_4_), channel_id=1, source_target_pairs={{0,6},{1,7},{2,0},{3,1},{4,2},{5,3},{6,4},{7,5},{8,14},{9,15},{10,... | collective-permute-start | bytes 196616 | tf_op jit(solution)/shard_map/ppermute | solution.py:484
  113.1 4.7 %collective-permute-start.11 = (bf16[128,256]{1,0:T(8,128)(2,1)S(1)}, bf16[128,256]{1,0:T(8,128)(2,1)S(1)}, u32[]{:S(2)}, u32[]{:S(2)}) collective-permute-start(bf16[128,256]{1,0:T(8,128)(2,1)S(1)} %residual.2.refs_4_), channel_id=1, source_target_pairs={{0,4},{1,5},{2,6},{3,7},{4,0},{5,1},{6,2},{7,3},{8,12},{9,13},{10,... | collective-permute-start | bytes 196616 | tf_op jit(solution)/shard_map/ppermute | solution.py:484
  113.2 5.0 %collective-permute-start.10 = (bf16[128,256]{1,0:T(8,128)(2,1)S(1)}, bf16[128,256]{1,0:T(8,128)(2,1)S(1)}, u32[]{:S(2)}, u32[]{:S(2)}) collective-permute-start(bf16[128,256]{1,0:T(8,128)(2,1)S(1)} %residual.2.refs_4_), channel_id=1, source_target_pairs={{0,2},{1,3},{2,4},{3,5},{4,6},{5,7},{6,0},{7,1},{8,10},{9,11},{10,... | collective-permute-start | bytes 196616 | tf_op jit(solution)/shard_map/ppermute | solution.py:484
  118.3 4.5 %collective-permute-start.13 = (bf16[4,128,256]{2,1,0:T(8,128)(2,1)S(1)}, bf16[4,128,256]{2,1,0:T(8,128)(2,1)S(1)}, u32[]{:S(2)}, u32[]{:S(2)}) collective-permute-start(bf16[4,128,256]{2,1,0:T(8,128)(2,1)S(1)} %pad_maximum_fusion.near_ref), channel_id=1, source_target_pairs={{0,1},{1,0},{2,3},{3,2},{4,5},{5,4},{6,7},{7,6},{8,9},{9,8},{10,11... | collective-permute-start | bytes 786440 | tf_op jit(solution)/shard_map/ppermute | solution.py:479
  124.1 34.2 %copy-start.1 = (s32[2,2048,128]{2,1,0:T(8,128)S(1)}, s32[2,2048,128]{2,1,0:T(8,128)}, u32[]{:S(2)}) copy-start(s32[2,2048,128]{2,1,0:T(8,128)} %words_ref.1) | copy-start | bytes 6291460
  124.1 34.2 %copy-start.5 = (bf16[256,2048]{1,0:T(8,128)(2,1)S(1)}, bf16[256,2048]{1,0:T(8,128)(2,1)}, u32[]{:S(2)}) copy-start(bf16[256,2048]{1,0:T(8,128)(2,1)} %wo_ref.1) | copy-start | bytes 3145732
  161.2 3.0 %collective-permute-start.14 = (bf16[4,128,256]{2,1,0:T(8,128)(2,1)S(1)}, bf16[4,128,256]{2,1,0:T(8,128)(2,1)S(1)}, u32[]{:S(2)}, u32[]{:S(2)}) collective-permute-start(bf16[4,128,256]{2,1,0:T(8,128)(2,1)S(1)} %get-tuple-element.81), channel_id=1, source_target_pairs={{0,1},{1,0},{2,3},{3,2},{4,5},{5,4},{6,7},{7,6},{8,9},{9,8},{10,11... | collective-permute-start | bytes 786440 | tf_op jit(solution)/shard_map/ppermute | solution.py:479
  164.8 6.2 %collective-permute-start.15 = (bf16[128,256]{1,0:T(8,128)(2,1)S(1)}, bf16[128,256]{1,0:T(8,128)(2,1)S(1)}, u32[]{:S(2)}, u32[]{:S(2)}) collective-permute-start(bf16[128,256]{1,0:T(8,128)(2,1)S(1)} %get-tuple-element.86), channel_id=1, source_target_pairs={{0,2},{1,3},{2,4},{3,5},{4,6},{5,7},{6,0},{7,1},{8,10},{9,11},{10,... | collective-permute-start | bytes 196616 | tf_op jit(solution)/shard_map/ppermute | solution.py:484
  164.9 6.1 %collective-permute-start.16 = (bf16[128,256]{1,0:T(8,128)(2,1)S(1)}, bf16[128,256]{1,0:T(8,128)(2,1)S(1)}, u32[]{:S(2)}, u32[]{:S(2)}) collective-permute-start(bf16[128,256]{1,0:T(8,128)(2,1)S(1)} %get-tuple-element.87), channel_id=1, source_target_pairs={{0,4},{1,5},{2,6},{3,7},{4,0},{5,1},{6,2},{7,3},{8,12},{9,13},{10,... | collective-permute-start | bytes 196616 | tf_op jit(solution)/shard_map/ppermute | solution.py:484
  166.6 4.4 %collective-permute-start.17 = (bf16[128,256]{1,0:T(8,128)(2,1)S(1)}, bf16[128,256]{1,0:T(8,128)(2,1)S(1)}, u32[]{:S(2)}, u32[]{:S(2)}) collective-permute-start(bf16[128,256]{1,0:T(8,128)(2,1)S(1)} %get-tuple-element.88), channel_id=1, source_target_pairs={{0,6},{1,7},{2,0},{3,1},{4,2},{5,3},{6,4},{7,5},{8,14},{9,15},{10,... | collective-permute-start | bytes 196616 | tf_op jit(solution)/shard_map/ppermute | solution.py:484

commit v3 on v1

--- a/solution.py
+++ b/solution.py
@@ -502,13 +502,19 @@
     return quad
 
 
-def pass_on(quad, seq_index, seq_count):
+def pass_on(quad, seq_count):
     size = quad.shape[0]
-    mine = quad[size - 1]
+    arrived = []
     for j in range(size - 1):
         pairs = [(k + size - 1, k + j) for k in range(0, seq_count, size)]
-        got = lax.ppermute(quad[j], "seq", pairs)
-        mine = jnp.where(seq_index % size == j, got, mine)
+        arrived.append(lax.ppermute(quad[j], "seq", pairs))
+    return arrived + [quad[size - 1]]
+
+
+def choose(arrived, place):
+    mine = arrived[-1]
+    for j, got in enumerate(arrived[:-1]):
+        mine = jnp.where(place == j, got, mine)
     return mine
 
 
@@ -551,10 +557,11 @@
     parts = cross_attention(where, queries, keys, values, cross_keep, root)
     pair, parts = lax.optimization_barrier((pair, parts))
     parts = exchange(parts, "seq")
-    inputs = pass_on(pair, seq_index, seq_count)
-    parts, inputs = lax.optimization_barrier((parts, inputs))
+    parts, *arrived = lax.optimization_barrier((parts, *pass_on(pair, seq_count)))
     pairs = head_count // 2
     own, theirs = combine(where, parts, wo_cross, pairs)
+    theirs, *arrived = lax.optimization_barrier((theirs, *arrived))
+    inputs = choose(arrived, seq_index % spread_size)
     latents = residual(where, head_sum(where, own, theirs), inputs, residual_keep, 0)
     near = jnp.stack([latents] + [along_chips(latents, d) for d in range(1, pairs)])
     far = to_partner(near)

time: 168 us -> 170 us (1.012)
    unnamed x16 -> x20, local copies, waits for them, and re-layouts: 1.64 us -> 3.44 us
  transfers between devices with their start and end apart: 21 -> 21, of which waited for: 13 -> 13; matrix products, arithmetic and copies ran while one was open for 2% -> 1% of each run, Pallas kernels for 15% -> 15%
where the time goes in v3:
time: 170 us; the launch traced here: 169 us
  waiting for transfers between devices  46.2 us (27%)
  starting transfers between devices  44.1 us (26%)
  Pallas kernels  38.2 us (22%)
  blocking collectives  33.2 us (20%)
  local copies, waits for them, and re-layouts  5.83 us (3%)
    all_to_all x1, blocking collectives, exchange(): return lax.all_to_all(value, axis, 0, 0, tiled=True)  33.2 us
    all_to_all x3, starting transfers between devices, exchange(): return lax.all_to_all(value, axis, 0, 0, tiled=True)  20.6 us
    all_to_all x3, waiting for transfers between devices, exchange(): return lax.all_to_all(value, axis, 0, 0, tiled=True)  20.5 us
    pallas_call x1, Pallas kernels, cross_attention(): pl.pallas_call(lambda *refs: cross_kernel(root, n, count // n, *refs), gr...  16.5 us
    ppermute x3, waiting for transfers between devices, pass_on(): arrived.append(lax.ppermute(quad[j], 'seq', pairs))  13.7 us
    ppermute x9, starting transfers between devices, along_chips(): lax.ppermute(value, 'head', [(i, (i + 2 * distance) % count) for i in ran...  11.2 us
    ppermute x9, waiting for transfers between devices, along_chips(): lax.ppermute(value, 'head', [(i, (i + 2 * distance) % count) for i in ran...  8.61 us
    pallas_call x1, Pallas kernels, keys_values(): pl.pallas_call(kv_kernel, grid=(tok_rows // block,), in_specs=[pl.BlockSp...  8.48 us
  transfers between devices with their start and end apart: 21, of which 13 were waited for; matrix products, arithmetic and copies ran while one was open for 1% of the time, Pallas kernels for 15%

profile of v3, /device:TPU:1, one launch (start us, length us, event | category | flops | bytes accessed | tf_op | source)
XLA Modules:
  0.0 168.9 jit_solution(9185000511368041882)
XLA Ops:
  0.1 3.9 %queries.1 = bf16[16,128,256]{2,1,0:T(8,128)(2,1)} custom-call(s32[2]{0:T(128)S(1)} %pad_add_fusion.refs_0_.where_ref, bf16[2048,2048]{1,0:T(8,128)(2,1)} %x_ref.1, bf16[2048,256]{1,0:T(8,128)(2,1)} %refs_2_.1), custom_call_target="tpu_custom_call" | custom-call | tf_op jit(solution)/shard_map/queries/pallas_call | solution.py:58
  4.0 11.5 %all-to-all-start = ((bf16[16,128,256]{2,1,0:T(8,128)(2,1)}), bf16[16,128,256]{2,1,0:T(8,128)(2,1)S(1)}, u32[]{:S(2)}, u32[]{:S(2)}) async-start(bf16[16,128,256]{2,1,0:T(8,128)(2,1)} %queries.1), calls=%async_computation | async-start | bytes 2097152 | tf_op jit(solution)/shard_map/all_to_all | solution.py:474
  15.5 8.5 %keys_values.1 = (bf16[2048,256]{1,0:T(8,128)(2,1)S(1)}, bf16[2048,256]{1,0:T(8,128)(2,1)}) custom-call(bf16[2048,2048]{1,0:T(8,128)(2,1)} %x_ref.1, bf16[2048,256]{1,0:T(8,128)(2,1)} %wk_ref.2, bf16[2048,256]{1,0:T(8,128)(2,1)} %wv_ref.2), custom_call_target="tpu_custom_call" | custom-call | tf_op jit(solution)/shard_map/keys_values/pallas_call | solution.py:78
  25.0 1.3 fusion
  26.3 5.3 %all-to-all-done = bf16[16,128,256]{2,1,0:T(8,128)(2,1)S(1)} async-done(((bf16[16,128,256]{2,1,0:T(8,128)(2,1)}), bf16[16,128,256]{2,1,0:T(8,128)(2,1)S(1)}, u32[]{:S(2)}, u32[]{:S(2)}) %all-to-all-start) | async-done | bytes 1048608 | tf_op jit(solution)/shard_map/all_to_all | solution.py:474
  31.6 1.1 broadcast_in_dim.2
  32.7 4.2 %all-to-all-start.1 = ((bf16[16,128,256]{2,1,0:T(8,128)(2,1)}), bf16[16,128,256]{2,1,0:T(8,128)(2,1)S(1)}, u32[]{:S(2)}, u32[]{:S(2)}) async-start(bf16[16,128,256]{2,1,0:T(8,128)(2,1)} %broadcast_in_dim.2), calls=%async_computation.1 | async-start | bytes 2097152 | tf_op jit(solution)/shard_map/all_to_all | solution.py:474
  36.9 15.1 %all-to-all-done.1.refs_1_ = bf16[16,128,256]{2,1,0:T(8,128)(2,1)S(1)} async-done(((bf16[16,128,256]{2,1,0:T(8,128)(2,1)}), bf16[16,128,256]{2,1,0:T(8,128)(2,1)S(1)}, u32[]{:S(2)}, u32[]{:S(2)}) %all-to-all-start.1) | async-done | bytes 1048608 | tf_op jit(solution)/shard_map/all_to_all | solution.py:474
  54.1 16.5 %cross_attention.1 = bf16[16,272,128]{2,1,0:T(8,128)(2,1)} custom-call(s32[2]{0:T(128)S(1)} %pad_add_fusion.refs_0_.where_ref, bf16[16,128,256]{2,1,0:T(8,128)(2,1)S(1)} %all-to-all-done.1.refs_1_, bf16[2048,256]{1,0:T(8,128)(2,1)} %copy-done.8, bf16[2048,256]{1,0:T(8,128)(2,1)} %get-tuple-element.62.refs_3_, s32[2,2048,256]{2,1,0:T(8,128)} %refs_4_.1), custom_call_target="tpu_custom_call" | custom-call | flops 4294967296 | bytes 4194304 | tf_op jit(solution)/shard_map/cross_attention/pallas_call | solution.py:233
  70.7 4.9 %all-to-all-start.2 = ((bf16[16,272,128]{2,1,0:T(8,128)(2,1)}), bf16[16,272,128]{2,1,0:T(8,128)(2,1)S(1)}, u32[]{:S(2)}, u32[]{:S(2)}) async-start(bf16[16,272,128]{2,1,0:T(8,128)(2,1)} %cross_attention.1), calls=%async_computation.2 | async-start | bytes 2228224 | tf_op jit(solution)/shard_map/all_to_all | solution.py:474
  75.6 1.4 collective-permute-start.3
  77.0 1.3 collective-permute-start.4
  79.0 13.7 %collective-permute-done.3 = bf16[128,256]{1,0:T(8,128)(2,1)} collective-permute-done((bf16[128,256]{1,0:T(8,128)(2,1)S(1)}, bf16[128,256]{1,0:T(8,128)(2,1)}, u32[]{:S(2)}, u32[]{:S(2)}) %collective-permute-start.3) | collective-permute-done | bytes 65568 | tf_op jit(solution)/shard_map/ppermute | solution.py:510
  93.3 2.1 %combine.1 = (f32[4,128,256]{2,1,0:T(8,128)S(1)}, bf16[4,128,256]{2,1,0:T(8,128)(2,1)S(1)}) custom-call(s32[2]{0:T(128)S(1)} %pad_add_fusion.refs_0_.where_ref, bf16[16,272,128]{2,1,0:T(8,128)(2,1)S(1)} %all-to-all-done.2.parts_ref, bf16[256,2048]{1,0:T(8,128)(2,1)} %wo_hbm.1), custom_call_target="tpu_custom_call" | custom-call | tf_op jit(solution)/shard_map/combine/pallas_call | solution.py:300
  96.2 1.5 collective-permute-start.6
  97.7 1.2 collective-permute-done.6.got_ref
  100.5 1.4 collective-permute-start.7
  101.8 2.6 %collective-permute-start.8 = (bf16[128,256]{1,0:T(8,128)(2,1)S(1)}, bf16[128,256]{1,0:T(8,128)(2,1)S(1)}, u32[]{:S(2)}, u32[]{:S(2)}) collective-permute-start(bf16[128,256]{1,0:T(8,128)(2,1)S(1)} %get-tuple-element.75), channel_id=1, source_target_pairs={{0,4},{1,5},{2,6},{3,7},{4,0},{5,1},{6,2},{7,3},{8,12},{9,13},{10,... | collective-permute-start | bytes 196616 | tf_op jit(solution)/shard_map/ppermute | solution.py:484
  108.5 2.1 %collective-permute-start.12 = (bf16[128,256]{1,0:T(8,128)(2,1)S(1)}, bf16[128,256]{1,0:T(8,128)(2,1)S(1)}, u32[]{:S(2)}, u32[]{:S(2)}) collective-permute-start(bf16[128,256]{1,0:T(8,128)(2,1)S(1)} %residual.2.refs_4_), channel_id=1, source_target_pairs={{0,6},{1,7},{2,0},{3,1},{4,2},{5,3},{6,4},{7,5},{8,14},{9,15},{10,... | collective-permute-start | bytes 196616 | tf_op jit(solution)/shard_map/ppermute | solution.py:484
  111.2 1.2 collective-permute-done.12
  112.5 2.8 %collective-permute-done.11 = bf16[128,256]{1,0:T(8,128)(2,1)S(1)} collective-permute-done((bf16[128,256]{1,0:T(8,128)(2,1)S(1)}, bf16[128,256]{1,0:T(8,128)(2,1)S(1)}, u32[]{:S(2)}, u32[]{:S(2)}) %collective-permute-start.11) | collective-permute-done | bytes 65568 | tf_op jit(solution)/shard_map/ppermute | solution.py:484
  115.6 3.6 %collective-permute-start.13 = (bf16[4,128,256]{2,1,0:T(8,128)(2,1)S(1)}, bf16[4,128,256]{2,1,0:T(8,128)(2,1)S(1)}, u32[]{:S(2)}, u32[]{:S(2)}) collective-permute-start(bf16[4,128,256]{2,1,0:T(8,128)(2,1)S(1)} %pad_maximum_fusion.near_ref), channel_id=1, source_target_pairs={{0,1},{1,0},{2,3},{3,2},{4,5},{5,4},{6,7},{7,6},{8,9},{9,8},{10,11... | collective-permute-start | bytes 786440 | tf_op jit(solution)/shard_map/ppermute | solution.py:479
  119.2 1.2 collective-permute-done.13.far_ref
  120.4 1.3 latent_qkv.1
  121.7 33.2 %all_to_all.20.kv_ref = bf16[16,128,512]{2,1,0:T(8,128)(2,1)S(1)} all-to-all(bf16[16,128,512]{2,1,0:T(8,128)(2,1)S(1)} %get-tuple-element.82), channel_id=1, replica_groups=mesh['seq'=16,'head'=8] {'seq'}, dimensions={0} | all-to-all | bytes 4194304 | tf_op jit(solution)/shard_map/all_to_all | solution.py:474
  155.0 2.8 %latent_attention.1 = (f32[4,128,256]{2,1,0:T(8,128)S(1)}, bf16[4,128,256]{2,1,0:T(8,128)(2,1)S(1)}) custom-call(s32[2]{0:T(128)S(1)} %pad_add_fusion.refs_0_.where_ref, bf16[128,256]{1,0:T(8,128)(2,1)S(1)} %get-tuple-element.81.q_ref, bf16[16,128,512]{2,1,0:T(8,128)(2,1)S(1)} %all_to_all.20.kv_ref, s32[2,2048,128]{2,1,0:T(8,128)S(1)} %copy-done.1, ...), custom_call_target="tpu_custom_call" | custom-call | tf_op jit(solution)/shard_map/latent_attention/pallas_call | solution.py:464
  157.8 1.8 %collective-permute-start.14 = (bf16[4,128,256]{2,1,0:T(8,128)(2,1)S(1)}, bf16[4,128,256]{2,1,0:T(8,128)(2,1)S(1)}, u32[]{:S(2)}, u32[]{:S(2)}) collective-permute-start(bf16[4,128,256]{2,1,0:T(8,128)(2,1)S(1)} %get-tuple-element.84), channel_id=1, source_target_pairs={{0,1},{1,0},{2,3},{3,2},{4,5},{5,4},{6,7},{7,6},{8,9},{9,8},{10,11... | collective-permute-start | bytes 786440 | tf_op jit(solution)/shard_map/ppermute | solution.py:479
  159.7 1.2 collective-permute-done.14.got_ref
  161.5 1.7 %collective-permute-start.16 = (bf16[128,256]{1,0:T(8,128)(2,1)S(1)}, bf16[128,256]{1,0:T(8,128)(2,1)S(1)}, u32[]{:S(2)}, u32[]{:S(2)}) collective-permute-start(bf16[128,256]{1,0:T(8,128)(2,1)S(1)} %get-tuple-element.87), channel_id=1, source_target_pairs={{0,4},{1,5},{2,6},{3,7},{4,0},{5,1},{6,2},{7,3},{8,12},{9,13},{10,... | collective-permute-start | bytes 196616 | tf_op jit(solution)/shard_map/ppermute | solution.py:484
  163.2 1.6 collective-permute-start.17
  164.9 2.7 %collective-permute-done.15.refs_1_ = bf16[128,256]{1,0:T(8,128)(2,1)S(1)} collective-permute-done((bf16[128,256]{1,0:T(8,128)(2,1)S(1)}, bf16[128,256]{1,0:T(8,128)(2,1)S(1)}, u32[]{:S(2)}, u32[]{:S(2)}) %collective-permute-start.15) | collective-permute-done | bytes 65568 | tf_op jit(solution)/shard_map/ppermute | solution.py:484
  167.7 1.2 residual.3
  (49 shorter events, 12.7 us)
Async XLA Ops:
  4.0 27.6 %all-to-all-start = ((bf16[16,128,256]{2,1,0:T(8,128)(2,1)}), bf16[16,128,256]{2,1,0:T(8,128)(2,1)S(1)}, u32[]{:S(2)}, u32[]{:S(2)}) async-start(bf16[16,128,256]{2,1,0:T(8,128)(2,1)} %queries.1), calls=%async_computation | async-start | bytes 2097152 | tf_op jit(solution)/shard_map/all_to_all | solution.py:474
  24.0 1.0 copy-start.8
  32.7 19.4 %all-to-all-start.1 = ((bf16[16,128,256]{2,1,0:T(8,128)(2,1)}), bf16[16,128,256]{2,1,0:T(8,128)(2,1)S(1)}, u32[]{:S(2)}, u32[]{:S(2)}) async-start(bf16[16,128,256]{2,1,0:T(8,128)(2,1)} %broadcast_in_dim.2), calls=%async_computation.1 | async-start | bytes 2097152 | tf_op jit(solution)/shard_map/all_to_all | solution.py:474
  52.0 18.6 %collective-permute-start = (bf16[4,128,256]{2,1,0:T(8,128)(2,1)S(1)}, bf16[4,128,256]{2,1,0:T(8,128)(2,1)S(1)}, u32[]{:S(2)}, u32[]{:S(2)}) collective-permute-start(bf16[4,128,256]{2,1,0:T(8,128)(2,1)S(1)} %bitcast.24), channel_id=1, source_target_pairs={{120,88},{121,89},{122,90},{123,91},{124,92},{125,93},{126,94},{12... | collective-permute-start | bytes 786440 | tf_op jit(solution)/shard_map/ppermute | solution.py:500
  52.7 17.9 %collective-permute-start.1 = (bf16[4,128,256]{2,1,0:T(8,128)(2,1)S(1)}, bf16[4,128,256]{2,1,0:T(8,128)(2,1)S(1)}, u32[]{:S(2)}, u32[]{:S(2)}) collective-permute-start(bf16[4,128,256]{2,1,0:T(8,128)(2,1)S(1)} %bitcast.23), channel_id=1, source_target_pairs={{120,56},{121,57},{122,58},{123,59},{124,60},{125,61},{126,62},{12... | collective-permute-start | bytes 786440 | tf_op jit(solution)/shard_map/ppermute | solution.py:500
  53.4 17.2 %collective-permute-start.2 = (bf16[4,128,256]{2,1,0:T(8,128)(2,1)S(1)}, bf16[4,128,256]{2,1,0:T(8,128)(2,1)S(1)}, u32[]{:S(2)}, u32[]{:S(2)}) collective-permute-start(bf16[4,128,256]{2,1,0:T(8,128)(2,1)S(1)} %bitcast.22), channel_id=1, source_target_pairs={{120,24},{121,25},{122,26},{123,27},{124,28},{125,29},{126,30},{12... | collective-permute-start | bytes 786440 | tf_op jit(solution)/shard_map/ppermute | solution.py:500
  70.7 22.0 %all-to-all-start.2 = ((bf16[16,272,128]{2,1,0:T(8,128)(2,1)}), bf16[16,272,128]{2,1,0:T(8,128)(2,1)S(1)}, u32[]{:S(2)}, u32[]{:S(2)}) async-start(bf16[16,272,128]{2,1,0:T(8,128)(2,1)} %cross_attention.1), calls=%async_computation.2 | async-start | bytes 2228224 | tf_op jit(solution)/shard_map/all_to_all | solution.py:474
  75.6 32.3 %copy-start = (s32[2,2048,128]{2,1,0:T(8,128)S(1)}, s32[2,2048,128]{2,1,0:T(8,128)}, u32[]{:S(2)}) copy-start(s32[2,2048,128]{2,1,0:T(8,128)} %refs_5_.3) | copy-start | bytes 6291460
  75.6 17.0 %collective-permute-start.3 = (bf16[128,256]{1,0:T(8,128)(2,1)S(1)}, bf16[128,256]{1,0:T(8,128)(2,1)}, u32[]{:S(2)}, u32[]{:S(2)}) collective-permute-start(bf16[128,256]{1,0:T(8,128)(2,1)S(1)} %get-tuple-element.96), channel_id=1, source_target_pairs={{24,0},{56,32},{88,64},{120,96},{25,1},{57,33},{89,65},{121,97},{2... | collective-permute-start | bytes 196616 | tf_op jit(solution)/shard_map/ppermute | solution.py:510
  77.0 15.6 %collective-permute-start.4 = (bf16[128,256]{1,0:T(8,128)(2,1)S(1)}, bf16[128,256]{1,0:T(8,128)(2,1)}, u32[]{:S(2)}, u32[]{:S(2)}) collective-permute-start(bf16[128,256]{1,0:T(8,128)(2,1)S(1)} %get-tuple-element.95), channel_id=1, source_target_pairs={{24,8},{56,40},{88,72},{120,104},{25,9},{57,41},{89,73},{121,105},... | collective-permute-start | bytes 196616 | tf_op jit(solution)/shard_map/ppermute | solution.py:510
  78.3 14.3 %collective-permute-start.5 = (bf16[128,256]{1,0:T(8,128)(2,1)S(1)}, bf16[128,256]{1,0:T(8,128)(2,1)S(1)}, u32[]{:S(2)}, u32[]{:S(2)}) collective-permute-start(bf16[128,256]{1,0:T(8,128)(2,1)S(1)} %get-tuple-element.94), channel_id=1, source_target_pairs={{24,16},{56,48},{88,80},{120,112},{25,17},{57,49},{89,81},{121,113... | collective-permute-start | bytes 196616 | tf_op jit(solution)/shard_map/ppermute | solution.py:510
  92.6 0.6 copy-start.9
  95.4 0.8 copy-start.6
  96.2 2.7 %collective-permute-start.6 = (bf16[4,128,256]{2,1,0:T(8,128)(2,1)S(1)}, bf16[4,128,256]{2,1,0:T(8,128)(2,1)S(1)}, u32[]{:S(2)}, u32[]{:S(2)}) collective-permute-start(bf16[4,128,256]{2,1,0:T(8,128)(2,1)S(1)} %get-tuple-element.72), channel_id=1, source_target_pairs={{0,1},{1,0},{2,3},{3,2},{4,5},{5,4},{6,7},{7,6},{8,9},{9,8},{10,11... | collective-permute-start | bytes 786440 | tf_op jit(solution)/shard_map/ppermute | solution.py:479
  98.8 1.0 copy-start.7
  99.9 20.5 %copy-start.2 = (bf16[2048,256]{1,0:T(8,128)(2,1)S(1)}, bf16[2048,256]{1,0:T(8,128)(2,1)}, u32[]{:S(2)}) copy-start(bf16[2048,256]{1,0:T(8,128)(2,1)} %wq_ref.1) | copy-start | bytes 3145732
  99.9 20.5 %copy-start.3 = (bf16[2048,256]{1,0:T(8,128)(2,1)S(1)}, bf16[2048,256]{1,0:T(8,128)(2,1)}, u32[]{:S(2)}) copy-start(bf16[2048,256]{1,0:T(8,128)(2,1)} %wk_ref.3) | copy-start | bytes 3145732
  99.9 20.5 %copy-start.4 = (bf16[2048,256]{1,0:T(8,128)(2,1)S(1)}, bf16[2048,256]{1,0:T(8,128)(2,1)}, u32[]{:S(2)}) copy-start(bf16[2048,256]{1,0:T(8,128)(2,1)} %wv_ref.3) | copy-start | bytes 3145732
  100.5 5.9 %collective-permute-start.7 = (bf16[128,256]{1,0:T(8,128)(2,1)S(1)}, bf16[128,256]{1,0:T(8,128)(2,1)S(1)}, u32[]{:S(2)}, u32[]{:S(2)}) collective-permute-start(bf16[128,256]{1,0:T(8,128)(2,1)S(1)} %get-tuple-element.74), channel_id=1, source_target_pairs={{0,2},{1,3},{2,4},{3,5},{4,6},{5,7},{6,0},{7,1},{8,10},{9,11},{10,... | collective-permute-start | bytes 196616 | tf_op jit(solution)/shard_map/ppermute | solution.py:484
  101.8 5.5 %collective-permute-start.8 = (bf16[128,256]{1,0:T(8,128)(2,1)S(1)}, bf16[128,256]{1,0:T(8,128)(2,1)S(1)}, u32[]{:S(2)}, u32[]{:S(2)}) collective-permute-start(bf16[128,256]{1,0:T(8,128)(2,1)S(1)} %get-tuple-element.75), channel_id=1, source_target_pairs={{0,4},{1,5},{2,6},{3,7},{4,0},{5,1},{6,2},{7,3},{8,12},{9,13},{10,... | collective-permute-start | bytes 196616 | tf_op jit(solution)/shard_map/ppermute | solution.py:484
  104.5 3.4 %collective-permute-start.9 = (bf16[128,256]{1,0:T(8,128)(2,1)S(1)}, bf16[128,256]{1,0:T(8,128)(2,1)S(1)}, u32[]{:S(2)}, u32[]{:S(2)}) collective-permute-start(bf16[128,256]{1,0:T(8,128)(2,1)S(1)} %get-tuple-element.76), channel_id=1, source_target_pairs={{0,6},{1,7},{2,0},{3,1},{4,2},{5,3},{6,4},{7,5},{8,14},{9,15},{10,... | collective-permute-start | bytes 196616 | tf_op jit(solution)/shard_map/ppermute | solution.py:484
  108.5 4.0 %collective-permute-start.12 = (bf16[128,256]{1,0:T(8,128)(2,1)S(1)}, bf16[128,256]{1,0:T(8,128)(2,1)S(1)}, u32[]{:S(2)}, u32[]{:S(2)}) collective-permute-start(bf16[128,256]{1,0:T(8,128)(2,1)S(1)} %residual.2.refs_4_), channel_id=1, source_target_pairs={{0,6},{1,7},{2,0},{3,1},{4,2},{5,3},{6,4},{7,5},{8,14},{9,15},{10,... | collective-permute-start | bytes 196616 | tf_op jit(solution)/shard_map/ppermute | solution.py:484
  110.5 4.7 %collective-permute-start.11 = (bf16[128,256]{1,0:T(8,128)(2,1)S(1)}, bf16[128,256]{1,0:T(8,128)(2,1)S(1)}, u32[]{:S(2)}, u32[]{:S(2)}) collective-permute-start(bf16[128,256]{1,0:T(8,128)(2,1)S(1)} %residual.2.refs_4_), channel_id=1, source_target_pairs={{0,4},{1,5},{2,6},{3,7},{4,0},{5,1},{6,2},{7,3},{8,12},{9,13},{10,... | collective-permute-start | bytes 196616 | tf_op jit(solution)/shard_map/ppermute | solution.py:484
  110.5 5.0 %collective-permute-start.10 = (bf16[128,256]{1,0:T(8,128)(2,1)S(1)}, bf16[128,256]{1,0:T(8,128)(2,1)S(1)}, u32[]{:S(2)}, u32[]{:S(2)}) collective-permute-start(bf16[128,256]{1,0:T(8,128)(2,1)S(1)} %residual.2.refs_4_), channel_id=1, source_target_pairs={{0,2},{1,3},{2,4},{3,5},{4,6},{5,7},{6,0},{7,1},{8,10},{9,11},{10,... | collective-permute-start | bytes 196616 | tf_op jit(solution)/shard_map/ppermute | solution.py:484
  115.6 4.8 %collective-permute-start.13 = (bf16[4,128,256]{2,1,0:T(8,128)(2,1)S(1)}, bf16[4,128,256]{2,1,0:T(8,128)(2,1)S(1)}, u32[]{:S(2)}, u32[]{:S(2)}) collective-permute-start(bf16[4,128,256]{2,1,0:T(8,128)(2,1)S(1)} %pad_maximum_fusion.near_ref), channel_id=1, source_target_pairs={{0,1},{1,0},{2,3},{3,2},{4,5},{5,4},{6,7},{7,6},{8,9},{9,8},{10,11... | collective-permute-start | bytes 786440 | tf_op jit(solution)/shard_map/ppermute | solution.py:479
  121.7 33.3 %copy-start.1 = (s32[2,2048,128]{2,1,0:T(8,128)S(1)}, s32[2,2048,128]{2,1,0:T(8,128)}, u32[]{:S(2)}) copy-start(s32[2,2048,128]{2,1,0:T(8,128)} %words_ref.1) | copy-start | bytes 6291460
  121.7 33.3 %copy-start.5 = (bf16[256,2048]{1,0:T(8,128)(2,1)S(1)}, bf16[256,2048]{1,0:T(8,128)(2,1)}, u32[]{:S(2)}) copy-start(bf16[256,2048]{1,0:T(8,128)(2,1)} %wo_ref.1) | copy-start | bytes 3145732
  157.8 3.0 %collective-permute-start.14 = (bf16[4,128,256]{2,1,0:T(8,128)(2,1)S(1)}, bf16[4,128,256]{2,1,0:T(8,128)(2,1)S(1)}, u32[]{:S(2)}, u32[]{:S(2)}) collective-permute-start(bf16[4,128,256]{2,1,0:T(8,128)(2,1)S(1)} %get-tuple-element.84), channel_id=1, source_target_pairs={{0,1},{1,0},{2,3},{3,2},{4,5},{5,4},{6,7},{7,6},{8,9},{9,8},{10,11... | collective-permute-start | bytes 786440 | tf_op jit(solution)/shard_map/ppermute | solution.py:479
  161.4 6.2 %collective-permute-start.15 = (bf16[128,256]{1,0:T(8,128)(2,1)S(1)}, bf16[128,256]{1,0:T(8,128)(2,1)S(1)}, u32[]{:S(2)}, u32[]{:S(2)}) collective-permute-start(bf16[128,256]{1,0:T(8,128)(2,1)S(1)} %get-tuple-element.86), channel_id=1, source_target_pairs={{0,2},{1,3},{2,4},{3,5},{4,6},{5,7},{6,0},{7,1},{8,10},{9,11},{10,... | collective-permute-start | bytes 196616 | tf_op jit(solution)/shard_map/ppermute | solution.py:484
  161.5 6.1 %collective-permute-start.16 = (bf16[128,256]{1,0:T(8,128)(2,1)S(1)}, bf16[128,256]{1,0:T(8,128)(2,1)S(1)}, u32[]{:S(2)}, u32[]{:S(2)}) collective-permute-start(bf16[128,256]{1,0:T(8,128)(2,1)S(1)} %get-tuple-element.87), channel_id=1, source_target_pairs={{0,4},{1,5},{2,6},{3,7},{4,0},{5,1},{6,2},{7,3},{8,12},{9,13},{10,... | collective-permute-start | bytes 196616 | tf_op jit(solution)/shard_map/ppermute | solution.py:484
  163.2 4.4 %collective-permute-start.17 = (bf16[128,256]{1,0:T(8,128)(2,1)S(1)}, bf16[128,256]{1,0:T(8,128)(2,1)S(1)}, u32[]{:S(2)}, u32[]{:S(2)}) collective-permute-start(bf16[128,256]{1,0:T(8,128)(2,1)S(1)} %get-tuple-element.88), channel_id=1, source_target_pairs={{0,6},{1,7},{2,0},{3,1},{4,2},{5,3},{6,4},{7,5},{8,14},{9,15},{10,... | collective-permute-start | bytes 196616 | tf_op jit(solution)/shard_map/ppermute | solution.py:484
